TPU v7x, 32 devices: a whole 2x2x4 slice. The times are simulated.
32 devices in a mesh: rep: 8 (over y, x, core), shard: 4 (over z).
Axes of the slice: x: 2, y: 2, z: 4, core: 2. Of those that a mesh axis runs over, the one named last changes fastest.
Arguments:
- deltas: bfloat16 [8, 512, 4096], P('rep', 'shard'), may hold values from -6 to 6
- presence: int32 [8], replicated, may hold values from 0 to 1, as said below
- owner_of: int32 [8], replicated, may hold values from 0 to 7, each once
- outer_params: float32 [512, 4096], P('shard', 'rep'), may hold values from -6 to 6
- momentum: float32 [512, 4096], P('shard', 'rep'), may hold values from -4 to 4
Outputs:
- new_weights: bfloat16 [512, 4096], P('shard')
- new_outer: float32 [512, 4096], P('shard', 'rep')
- new_momentum: float32 [512, 4096], P('shard', 'rep')
Inputs may be any that keep to these rules, and one draw needn't show every extreme that they name: `presence`: at least one replica group is present.
All inputs are finite; a program needn't handle non-finite values.
Results may differ from a plain program's by a relative error of at most 0.0075.
Values may be sent and summed in bfloat16 or wider, within the bound.
No kernel may reach another device: no remote copies, remote signals or barrier semaphores. Data moves between devices by JAX's collectives and lax.ppermute only.
A program may use at most 64 MiB of HBM per device.

v0:
```python
import jax
import jax.numpy as jnp
from jax import lax
from jax.sharding import PartitionSpec as P


def shards(deltas, presence, owner_of, outer_params, momentum):
    groups = lax.axis_size("rep")
    rows = deltas.shape[1]
    width = deltas.shape[2] // groups
    present = presence.astype(jnp.float32)
    count = jnp.sum(present)
    local_blocks = deltas[0].reshape(rows, groups, width)
    slotted = jnp.take(local_blocks, owner_of, axis=1).reshape(rows, groups * width)
    own_flag = lax.dynamic_index_in_dim(present, lax.axis_index("rep"), 0, keepdims=False)
    term = slotted.astype(jnp.float32) * own_flag
    total = lax.psum_scatter(
        term.astype(jnp.bfloat16), "rep", scatter_dimension=1, tiled=True
    ).astype(jnp.float32)
    average = total / count
    new_momentum = 0.9 * momentum + average
    new_outer = outer_params - 0.7 * (average + 0.9 * new_momentum)
    shipped = new_outer.astype(jnp.bfloat16)
    gathered = lax.all_gather(shipped, "rep", axis=1, tiled=True)
    inverse = jnp.argsort(owner_of)
    natural = jnp.take(gathered.reshape(rows, groups, width), inverse, axis=1)
    new_weights = natural.reshape(rows, groups * width)
    return (new_weights, new_outer, new_momentum)


def solution(mesh):
    return jax.shard_map(
        shards,
        mesh=mesh,
        in_specs=(P("rep", "shard", None), P(), P(), P("shard", "rep"), P("shard", "rep")),
        out_specs=(P("shard", None), P("shard", "rep"), P("shard", "rep")),
        check_vma=False,
    )
```

profile of v0, /device:TPU:0, one launch (start us, length us, event | category | flops | bytes accessed | tf_op | source)
XLA Modules:
  0.0 90.7 jit_solution(5586122691734265856)
XLA Ops:
  7.2 0.7 compare_select_fusion.1
  7.9 0.7 compare_and_fusion.1
  8.5 0.7 convert_element_type.20
  9.2 1.6 %copy.8 = bf16[1,128,4096]{1,2,0:T(8,128)(2,1)S(1)} copy(bf16[1,128,4096]{2,1,0:T(8,128)(2,1)} %param.7) | data formatting | bytes 2097152 | tf_op args[0]
  10.8 0.5 copy.9
  11.4 0.6 dynamic_slice.4
  12.0 0.6 gather_fusion
  12.6 1.0 %multiply_convert_fusion = bf16[128,8,512]{2,0,1:T(8,128)(2,1)S(1)} fusion(bf16[8,128,512]{2,1,0:T(8,128)(2,1)S(1)} %gather_fusion, f32[]{:T(128)} %bitcast.2, pred[8]{0:T(512)(128)(4,1)S(1)} %compare_and_fusion.1), kind=kLoop, calls=%fused_computation.2 | loop fusion | flops 2097152 | bytes 2097164 | tf_op jit(solution)/shard_map/convert_element_type | solution.py:18
  13.5 1.3 %copy.10 = bf16[128,8,512]{0,2,1:T(8,128)(2,1)} copy(bf16[128,8,512]{2,0,1:T(8,128)(2,1)S(1)} %multiply_convert_fusion) | data formatting | bytes 2097152 | tf_op jit(solution)/shard_map/convert_element_type | solution.py:18
  14.9 0.9 copy-done
  15.8 0.1 copy.11
  16.0 0.1 copy.12
  16.1 0.6 convert_reduce_fusion
  16.7 37.1 %reduce-scatter.2.cloned.1.call-done = bf16[128,512]{0,1:T(8,128)(2,1)} async-done(((bf16[128,4096]{0,1:T(8,128)(2,1)}), bf16[128,512]{0,1:T(8,128)(2,1)}) %reduce-scatter.2.cloned.1.call-update) | async-done | bytes 131088 | tf_op jit(solution)/shard_map/reduce_scatter | solution.py:17
  53.7 2.3 %fusion = (bf16[128,512]{0,1:T(8,128)(2,1)}, f32[128,512]{0,1:T(8,128)S(1)}, f32[128,512]{0,1:T(8,128)S(1)}) fusion(f32[128,512]{0,1:T(8,128)S(1)} %copy.12, f32[128,512]{0,1:T(8,128)S(1)} %copy.11, f32[]{:T(128)} %convert_reduce_fusion, bf16[128,512]{0,1:T(8,128)(2,1)} %reduce-scatter.2.cloned.1.call-done), kind=kLoop, calls=%fused_computation.14 | loop fusion | flops 589824 | bytes 1310724 | tf_op jit(solution)/shard_map/convert_element_type | solution.py:23
  56.1 1.0 %sort.17 = (s32[8]{0:T(128)}, s32[8]{0:T(128)S(1)}) sort(s32[8]{0:T(128)S(1)} %copy-done.3, s32[8]{0:T(128)S(1)} %iota.4), dimensions={0}, to_apply=%region_2.4 | sort | flops 24 | bytes 128 | tf_op jit(solution)/shard_map/jit(argsort)/sort | solution.py:25
  57.1 0.8 copy.16
  57.9 0.8 copy.17
  58.7 20.9 %all-gather.2.cloned.1.call-done = bf16[128,4096]{0,1:T(8,128)(2,1)} async-done(((bf16[128,512]{0,1:T(8,128)(2,1)}), bf16[128,4096]{0,1:T(8,128)(2,1)}) %all-gather.2.cloned.1.call-update) | async-done | bytes 1048592 | tf_op jit(solution)/shard_map/all_gather | solution.py:24
  79.6 1.5 %copy.13 = bf16[128,8,512]{2,0,1:T(8,128)(2,1)S(1)} copy(bf16[128,8,512]{0,2,1:T(8,128)(2,1)} %bitcast.12) | data formatting | bytes 2097152 | tf_op jit(solution)/shard_map/reshape | solution.py:26
  81.1 0.6 gather_fusion.1
  81.7 0.2 select_bitcast_fusion
  81.9 0.7 copy.14
  82.6 1.3 %copy.15 = bf16[128,4096]{1,0:T(8,128)(2,1)} copy(bf16[128,4096]{0,1:T(8,128)(2,1)S(1)} %bitcast.10) | data formatting | bytes 2097152
  (16 shorter events, 0.2 us)
Async XLA Ops:
  7.2 46.6 %reduce-scatter.2.cloned.1.call-start = ((), (), s32[]{:S(2)}) async-start(), calls=%async_computation.1 | async-start | bytes 1179648 | tf_op jit(solution)/shard_map/reduce_scatter | solution.py:17
  14.8 0.9 %copy-start = (f32[128,512]{1,0:T(8,128)S(1)}, f32[128,512]{1,0:T(8,128)}, u32[]{:S(2)}) copy-start(f32[128,512]{1,0:T(8,128)} %param.11) | copy-start | bytes 786436
  14.9 1.1 %copy-start.1 = (f32[128,512]{1,0:T(8,128)S(1)}, f32[128,512]{1,0:T(8,128)}, u32[]{:S(2)}) copy-start(f32[128,512]{1,0:T(8,128)} %param.10) | copy-start | bytes 786436
  14.9 1.2 %copy-start.2 = (s32[8]{0:T(128)S(1)}, s32[8]{0:T(128)}, u32[]{:S(2)}) copy-start(s32[8]{0:T(128)} %param.8) | copy-start | bytes 100
  14.9 64.7 %all-gather.2.cloned.1.call-start = ((), (), s32[]{:S(2)}) async-start(), calls=%async_computation.2 | async-start | bytes 1179648 | tf_op jit(solution)/shard_map/all_gather | solution.py:24
  15.9 40.1 %copy-start.3 = (s32[8]{0:T(128)S(1)}, s32[8]{0:T(128)}, u32[]{:S(2)}) copy-start(s32[8]{0:T(128)} %param.9) | copy-start | bytes 100
Sparse Core Ops, SparseCore 0:
  15.0 38.6 reduce-scatter.1
  56.2 23.3 all-gather.1
where the time goes:
time: 91 us; the launch traced here: 90.7 us
  waiting for transfers between devices  58 us (64%)
  between operations  14.2 us (16%)
  local copies, waits for them, and re-layouts  11.5 us (13%)
  other arithmetic  6.97 us (8%)
    reduce_scatter x1, waiting for transfers between devices, shards(): lax.psum_scatter(term.astype(jnp.bfloat16), 'rep', scatter_dimension=1, t...  37.1 us
    all_gather x1, waiting for transfers between devices, shards(): gathered = lax.all_gather(shipped, 'rep', axis=1, tiled=True)  20.9 us
    unnamed x14, local copies, waits for them, and re-layouts  5.72 us
    convert_element_type x1, other arithmetic, shards(): shipped = new_outer.astype(jnp.bfloat16)  2.29 us
  transfers between devices with their start and end apart: 2, of which 2 were waited for; matrix products, arithmetic and copies ran while one was open for 4% of the time, Pallas kernels for 0%

commit v1 on v0

v1 whole, which is shorter than its diff:
```python
import jax
import jax.numpy as jnp
from jax import lax
from jax.sharding import PartitionSpec as P


def shards(deltas, presence, owner_of, outer_params, momentum):
    groups = lax.axis_size("rep")
    pair = 2 if groups % 2 == 0 else 1
    chips = groups // pair
    flips = chips & (chips - 1) == 0
    rows = deltas.shape[1]
    width = deltas.shape[2] // groups
    me = lax.axis_index("rep")
    chip, core = me // pair, me % pair

    def target(at, step):
        return at ^ step if flips else (at + step) % chips

    def origin(at, step):
        return at ^ step if flips else (at - step) % chips

    def across(x, step):
        return lax.ppermute(x, "rep", [(i, target(i // pair, step) * pair + i % pair) for i in range(groups)])

    def partner(x):
        return lax.ppermute(x, "rep", [(i, i ^ 1) for i in range(groups)])

    def block(index):
        return lax.dynamic_slice(deltas[0], (0, owner_of[index] * width), (rows, width))

    present = presence.astype(jnp.float32)
    count = jnp.sum(present)
    own_flag = present[me]
    sums = [block(target(chip, s) * pair + core).astype(jnp.float32) * own_flag for s in range(chips)]
    if pair == 2:
        sent = jnp.stack([block(target(chip, s) * pair + 1 - core) for s in range(chips)])
        other = partner(sent)
        other_flag = present[me ^ 1]
        sums = [a + other[s].astype(jnp.float32) * other_flag for s, a in enumerate(sums)]
    total = sums[0]
    for s in range(1, chips):
        total = total + across(sums[s].astype(jnp.bfloat16), s).astype(jnp.float32)
    average = total / count
    new_momentum = 0.9 * momentum + average
    new_outer = outer_params - 0.7 * (average + 0.9 * new_momentum)
    shipped = new_outer.astype(jnp.bfloat16)
    got = jnp.stack([shipped] + [across(shipped, s) for s in range(1, chips)])
    parts = [(core, got)]
    if pair == 2:
        parts.append((1 - core, partner(got)))
    new_weights = jnp.zeros((rows, groups * width), jnp.bfloat16)
    for from_core, held in parts:
        for s in range(chips):
            at = owner_of[origin(chip, s) * pair + from_core] * width
            new_weights = lax.dynamic_update_slice(new_weights, held[s], (0, at))
    return (new_weights, new_outer, new_momentum)


def solution(mesh):
    return jax.shard_map(
        shards,
        mesh=mesh,
        in_specs=(P("rep", "shard", None), P(), P(), P("shard", "rep"), P("shard", "rep")),
        out_specs=(P("shard", None), P("shard", "rep"), P("shard", "rep")),
        check_vma=False,
    )
```

time: 91 us -> 38.5 us (0.42)
  waiting for transfers between devices: 58 us -> 11.5 us
  starting transfers between devices: 0.08 us -> 8.21 us
  local copies, waits for them, and re-layouts: 11.5 us -> 5.02 us
  between operations: 14.2 us -> 8.49 us
  other arithmetic: 6.97 us -> 4.98 us
    reduce_scatter x1 -> x0, waiting for transfers between devices: 37.1 us -> none  [shards(): lax.psum_scatter(term.astype(jnp.bfloat16), 'rep', scatter_dimension=1, t...]
    all_gather x1 -> x0, waiting for transfers between devices: 20.9 us -> none  [shards(): gathered = lax.all_gather(shipped, 'rep', axis=1, tiled=True)]
    ppermute x0 -> x8, waiting for transfers between devices: none -> 11.5 us  [the longest x6 11.5 us: across(): lax.ppermute(x, 'rep', [(i, target(i // pair, step) * pair + i % pair) fo...]
    ppermute x0 -> x8, starting transfers between devices: none -> 8.21 us  [the longest x6 7.58 us: across(): lax.ppermute(x, 'rep', [(i, target(i // pair, step) * pair + i % pair) fo...]
    unnamed x14 -> x12, local copies, waits for them, and re-layouts: 5.72 us -> 2.28 us
    dynamic_update_slice x0 -> x1, other arithmetic: none -> 2.83 us  [shards(): new_weights = lax.dynamic_update_slice(new_weights, held[s], (0, at))]
    dynamic_slice x1 -> x3, local copies, waits for them, and re-layouts: 0.59 us -> 2.54 us  [the longest x1 1.23 us: block(): lax.dynamic_slice(deltas[0], (0, owner_of[index] * width), (rows, width))]
    convert_element_type x2 -> x1, other arithmetic: 3.25 us -> 1.33 us  [shards(): total = total + across(sums[s].astype(jnp.bfloat16), s).astype(jnp.float32)]
  transfers between devices with their start and end apart: 2 -> 8, of which waited for: 2 -> 5; matrix products, arithmetic and copies ran while one was open for 4% -> 3% of each run, Pallas kernels for 0% -> 0%
where the time goes in v1:
time: 38.5 us; the launch traced here: 38.2 us
  waiting for transfers between devices  11.5 us (30%)
  between operations  8.49 us (22%)
  starting transfers between devices  8.21 us (21%)
  local copies, waits for them, and re-layouts  5.02 us (13%)
  other arithmetic  4.98 us (13%)
    ppermute x6, waiting for transfers between devices, across(): lax.ppermute(x, 'rep', [(i, target(i // pair, step) * pair + i % pair) fo...  11.5 us
    ppermute x6, starting transfers between devices, across(): lax.ppermute(x, 'rep', [(i, target(i // pair, step) * pair + i % pair) fo...  7.58 us
    dynamic_update_slice x1, other arithmetic, shards(): new_weights = lax.dynamic_update_slice(new_weights, held[s], (0, at))  2.83 us
    unnamed x12, local copies, waits for them, and re-layouts  2.28 us
    convert_element_type x1, other arithmetic, shards(): total = total + across(sums[s].astype(jnp.bfloat16), s).astype(jnp.float32)  1.33 us
    dynamic_slice x1, local copies, waits for them, and re-layouts, block(): lax.dynamic_slice(deltas[0], (0, owner_of[index] * width), (rows, width))  1.23 us
  transfers between devices with their start and end apart: 8, of which 5 were waited for; matrix products, arithmetic and copies ran while one was open for 3% of the time, Pallas kernels for 0%

profile of v1, /device:TPU:0, one launch (start us, length us, event | category | flops | bytes accessed | tf_op | source)
XLA Modules:
  0.0 38.2 jit_solution(15047342385828489263)
XLA Ops:
  0.7 0.6 %copy-done.4 = s32[8]{0:T(128)S(1)} copy-done((s32[8]{0:T(128)S(1)}, s32[8]{0:T(128)}, u32[]{:S(2)}) %copy-start.4) | copy-done | bytes 56
  1.4 0.7 %fusion.10 = (s32[1]{0:T(128)}, s32[1]{0:T(128)}, s32[1]{0:T(128)}, s32[1]{0:T(128)}, s32[1]{0:T(128)}, /*index=5*/s32[1]{0:T(128)}, s32[1]{0:T(128)}, s32[1]{0:...) fusion(s32[8]{0:T(128)S(1)} %copy-done.4, s32[]{:T(128)S(6)} %select_n.123, s32[]{:T(128)S(6)} %select_n.119, ...), kind=kLoop, calls=%fused_computation.31 | loop fusion | bytes 144 | tf_op jit(solution)/shard_map/dynamic_slice | solution.py:55
  4.6 1.2 %constant_dynamic-slice_fusion.3 = (bf16[1,128,512]{2,1,0:T(8,128)(2,1)S(1)}, bf16[1,128,512]{2,1,0:T(8,128)(2,1)S(1)}, bf16[1,128,512]{2,1,0:T(8,128)(2,1)S(1)}, bf16[1,128,512]{2,1,0:T(8,128)(2,1)S(1)}) fusion(bf16[1,128,4096]{2,1,0:T(8,128)(2,1)} %param.5, s32[]{:T(128)S(6)} %select_n.103, s32[]{:T(128)S(6)} %select_n.109, s32[]{:T(128)S(6)} %select_n.107, ...), kind=kLoop, calls=%fused_computation.29 | loop fusion | bytes 1048592 | tf_op jit(solution)/shard_map/dynamic_slice | solution.py:30
  5.8 0.1 pad_maximum_fusion
  5.9 0.6 %collective-permute-start = (bf16[4,128,512]{2,1,0:T(8,128)(2,1)S(1)}, bf16[4,128,512]{2,1,0:T(8,128)(2,1)S(1)}, u32[]{:S(2)}, u32[]{:S(2)}) collective-permute-start(bf16[4,128,512]{2,1,0:T(8,128)(2,1)S(1)} %pad_maximum_fusion), channel_id=1, source_target_pairs={{0,4},{4,0},{8,12},{12,8},{16,20},{20,16},{24,28},{28,24},{1,5},{5... | collective-permute-start | bytes 1572872 | tf_op jit(solution)/shard_map/ppermute | solution.py:27
  8.4 0.6 %copy-done.5 = s32[8]{0:T(128)S(1)} copy-done((s32[8]{0:T(128)S(1)}, s32[8]{0:T(128)}, u32[]{:S(2)}) %copy-start.5) | copy-done | bytes 56
  9.0 0.6 %fusion.11 = (f32[1]{0:T(128)}, f32[1]{0:T(128)}) fusion(f32[8]{0:T(128)S(1)} %convert_element_type.66, s32[]{:T(128)S(6)} %select_n.101, s32[]{:T(128)S(6)} %select_n.110), kind=kLoop, calls=%fused_computation.32 | loop fusion | bytes 24 | tf_op jit(solution)/shard_map/dynamic_slice | solution.py:34
  9.6 1.3 %fusion.3 = (bf16[128,512]{1,0:T(8,128)(2,1)S(1)}, bf16[128,512]{1,0:T(8,128)(2,1)S(1)}, bf16[128,512]{1,0:T(8,128)(2,1)S(1)}) fusion(bf16[4,128,512]{2,1,0:T(8,128)(2,1)S(1)} %collective-permute-done, bf16[1,128,4096]{2,1,0:T(8,128)(2,1)S(1)} %copy-done, s32[]{:T(128)S(6)} %select_n.112, f32[]{:T(128)} %bitcast.6, f32[]{:T(128)} %bitcast.1, ...), kind=kLoop, calls=%fused_computation.11 | loop fusion | flops 1179648 | bytes 1179668 | tf_op jit(solution)/shard_map/convert_element_type | solution.py:43
  11.0 2.6 %collective-permute-start.1 = (bf16[128,512]{1,0:T(8,128)(2,1)S(1)}, bf16[128,512]{1,0:T(8,128)(2,1)S(1)}, u32[]{:S(2)}, u32[]{:S(2)}) collective-permute-start(bf16[128,512]{1,0:T(8,128)(2,1)S(1)} %get-tuple-element.7), channel_id=1, source_target_pairs={{0,8},{4,12},{8,0},{12,4},{16,24},{20,28},{24,16},{28,20},{1,9},{5... | collective-permute-start | bytes 393224 | tf_op jit(solution)/shard_map/ppermute | solution.py:24
  13.5 1.5 %collective-permute-start.3 = (bf16[128,512]{1,0:T(8,128)(2,1)S(1)}, bf16[128,512]{1,0:T(8,128)(2,1)S(1)}, u32[]{:S(2)}, u32[]{:S(2)}) collective-permute-start(bf16[128,512]{1,0:T(8,128)(2,1)S(1)} %get-tuple-element.8), channel_id=1, source_target_pairs={{0,24},{4,28},{8,16},{12,20},{16,8},{20,12},{24,0},{28,4},{1,25},{... | collective-permute-start | bytes 393224 | tf_op jit(solution)/shard_map/ppermute | solution.py:24
  15.7 0.7 %convert_reduce_fusion = f32[]{:T(128)} fusion(s32[8]{0:T(128)S(1)} %copy-done.5), kind=kLoop, calls=%fused_computation.30 | loop fusion | flops 15 | bytes 36 | tf_op jit(solution)/shard_map/reduce_sum | solution.py:33
  16.4 1.4 %collective-permute-done.1 = bf16[128,512]{1,0:T(8,128)(2,1)S(1)} collective-permute-done((bf16[128,512]{1,0:T(8,128)(2,1)S(1)}, bf16[128,512]{1,0:T(8,128)(2,1)S(1)}, u32[]{:S(2)}, u32[]{:S(2)}) %collective-permute-start.1) | collective-permute-done | bytes 131104 | tf_op jit(solution)/shard_map/ppermute | solution.py:24
  17.9 3.9 %collective-permute-done.3 = bf16[128,512]{1,0:T(8,128)(2,1)S(1)} collective-permute-done((bf16[128,512]{1,0:T(8,128)(2,1)S(1)}, bf16[128,512]{1,0:T(8,128)(2,1)S(1)}, u32[]{:S(2)}, u32[]{:S(2)}) %collective-permute-start.3) | collective-permute-done | bytes 131104 | tf_op jit(solution)/shard_map/ppermute | solution.py:24
  21.8 1.4 %collective-permute-done.2 = bf16[128,512]{1,0:T(8,128)(2,1)S(1)} collective-permute-done((bf16[128,512]{1,0:T(8,128)(2,1)S(1)}, bf16[128,512]{1,0:T(8,128)(2,1)S(1)}, u32[]{:S(2)}, u32[]{:S(2)}) %collective-permute-start.2) | collective-permute-done | bytes 131104 | tf_op jit(solution)/shard_map/ppermute | solution.py:24
  23.1 0.1 broadcast_in_dim.3
  23.3 2.8 %constant_dynamic-update-slice_fusion.3 = (bf16[128,4096]{1,0:T(8,128)(2,1)S(1)}, bf16[128,512]{1,0:T(8,128)(2,1)S(1)}, f32[128,512]{1,0:T(8,128)}, f32[128,512]{1,0:T(8,128)}) fusion(bf16[128,4096]{1,0:T(8,128)(2,1)S(1)} %broadcast_in_dim.3, s32[]{:T(128)S(6)} %select_n.100, f32[128,512]{1,0:T(8,128)S(1)} %copy-done.2, f32[]{:T(128)} %convert_reduce_fusion, ...), kind=kLoop, calls=%fused_computation.25 | loop fusion | flops 1245184 | bytes 1966096 | tf_op jit(solution)/shard_map/dynamic_update_slice | solution.py:56
  26.1 1.4 %collective-permute-start.6 = (bf16[128,512]{1,0:T(8,128)(2,1)S(1)}, bf16[128,512]{1,0:T(8,128)(2,1)S(1)}, u32[]{:S(2)}, u32[]{:S(2)}) collective-permute-start(bf16[128,512]{1,0:T(8,128)(2,1)S(1)} %get-tuple-element.4), channel_id=1, source_target_pairs={{0,24},{4,28},{8,16},{12,20},{16,8},{20,12},{24,0},{28,4},{1,25},{... | collective-permute-start | bytes 393224 | tf_op jit(solution)/shard_map/ppermute | solution.py:24
  27.5 1.5 %collective-permute-start.5 = (bf16[128,512]{1,0:T(8,128)(2,1)S(1)}, bf16[128,512]{1,0:T(8,128)(2,1)S(1)}, u32[]{:S(2)}, u32[]{:S(2)}) collective-permute-start(bf16[128,512]{1,0:T(8,128)(2,1)S(1)} %get-tuple-element.4), channel_id=1, source_target_pairs={{0,16},{4,20},{8,24},{12,28},{16,0},{20,4},{24,8},{28,12},{1,17},{... | collective-permute-start | bytes 393224 | tf_op jit(solution)/shard_map/ppermute | solution.py:24
  29.1 0.5 %collective-permute-start.4 = (bf16[128,512]{1,0:T(8,128)(2,1)S(1)}, bf16[128,512]{1,0:T(8,128)(2,1)S(1)}, u32[]{:S(2)}, u32[]{:S(2)}) collective-permute-start(bf16[128,512]{1,0:T(8,128)(2,1)S(1)} %get-tuple-element.4), channel_id=1, source_target_pairs={{0,8},{4,12},{8,0},{12,4},{16,24},{20,28},{24,16},{28,20},{1,9},{5... | collective-permute-start | bytes 393224 | tf_op jit(solution)/shard_map/ppermute | solution.py:24
  29.6 3.4 %collective-permute-done.6 = bf16[128,512]{1,0:T(8,128)(2,1)S(1)} collective-permute-done((bf16[128,512]{1,0:T(8,128)(2,1)S(1)}, bf16[128,512]{1,0:T(8,128)(2,1)S(1)}, u32[]{:S(2)}, u32[]{:S(2)}) %collective-permute-start.6) | collective-permute-done | bytes 131104 | tf_op jit(solution)/shard_map/ppermute | solution.py:24
  33.0 1.4 %collective-permute-done.5 = bf16[128,512]{1,0:T(8,128)(2,1)S(1)} collective-permute-done((bf16[128,512]{1,0:T(8,128)(2,1)S(1)}, bf16[128,512]{1,0:T(8,128)(2,1)S(1)}, u32[]{:S(2)}, u32[]{:S(2)}) %collective-permute-start.5) | collective-permute-done | bytes 131104 | tf_op jit(solution)/shard_map/ppermute | solution.py:24
  34.4 0.1 pad_maximum_fusion.1
  34.4 0.1 collective-permute-start.7
  37.2 1.0 %copy-done.1 = bf16[128,4096]{1,0:T(8,128)(2,1)} copy-done((bf16[128,4096]{1,0:T(8,128)(2,1)}, bf16[128,4096]{1,0:T(8,128)(2,1)S(1)}, u32[]{:S(2)}) %copy-start.1) | copy-done | bytes 1048600
  (21 shorter events, 0.2 us)
Async XLA Ops:
  0.7 0.7 %copy-start.4 = (s32[8]{0:T(128)S(1)}, s32[8]{0:T(128)}, u32[]{:S(2)}) copy-start(s32[8]{0:T(128)} %param.7) | copy-start | bytes 100
  4.6 5.0 %copy-start = (bf16[1,128,4096]{2,1,0:T(8,128)(2,1)S(1)}, bf16[1,128,4096]{2,1,0:T(8,128)(2,1)}, u32[]{:S(2)}) copy-start(bf16[1,128,4096]{2,1,0:T(8,128)(2,1)} %param.5) | copy-start | bytes 3145732
  5.9 3.7 %collective-permute-start = (bf16[4,128,512]{2,1,0:T(8,128)(2,1)S(1)}, bf16[4,128,512]{2,1,0:T(8,128)(2,1)S(1)}, u32[]{:S(2)}, u32[]{:S(2)}) collective-permute-start(bf16[4,128,512]{2,1,0:T(8,128)(2,1)S(1)} %pad_maximum_fusion), channel_id=1, source_target_pairs={{0,4},{4,0},{8,12},{12,8},{16,20},{20,16},{24,28},{28,24},{1,5},{5... | collective-permute-start | bytes 1572872 | tf_op jit(solution)/shard_map/ppermute | solution.py:27
  8.3 0.7 %copy-start.5 = (s32[8]{0:T(128)S(1)}, s32[8]{0:T(128)}, u32[]{:S(2)}) copy-start(s32[8]{0:T(128)} %param.6) | copy-start | bytes 100
  11.0 6.9 %collective-permute-start.1 = (bf16[128,512]{1,0:T(8,128)(2,1)S(1)}, bf16[128,512]{1,0:T(8,128)(2,1)S(1)}, u32[]{:S(2)}, u32[]{:S(2)}) collective-permute-start(bf16[128,512]{1,0:T(8,128)(2,1)S(1)} %get-tuple-element.7), channel_id=1, source_target_pairs={{0,8},{4,12},{8,0},{12,4},{16,24},{20,28},{24,16},{28,20},{1,9},{5... | collective-permute-start | bytes 393224 | tf_op jit(solution)/shard_map/ppermute | solution.py:24
  13.5 8.3 %collective-permute-start.3 = (bf16[128,512]{1,0:T(8,128)(2,1)S(1)}, bf16[128,512]{1,0:T(8,128)(2,1)S(1)}, u32[]{:S(2)}, u32[]{:S(2)}) collective-permute-start(bf16[128,512]{1,0:T(8,128)(2,1)S(1)} %get-tuple-element.8), channel_id=1, source_target_pairs={{0,24},{4,28},{8,16},{12,20},{16,8},{20,12},{24,0},{28,4},{1,25},{... | collective-permute-start | bytes 393224 | tf_op jit(solution)/shard_map/ppermute | solution.py:24
  15.0 8.1 %collective-permute-start.2 = (bf16[128,512]{1,0:T(8,128)(2,1)S(1)}, bf16[128,512]{1,0:T(8,128)(2,1)S(1)}, u32[]{:S(2)}, u32[]{:S(2)}) collective-permute-start(bf16[128,512]{1,0:T(8,128)(2,1)S(1)} %get-tuple-element.9), channel_id=1, source_target_pairs={{0,16},{4,20},{8,24},{12,28},{16,0},{20,4},{24,8},{28,12},{1,17},{... | collective-permute-start | bytes 393224 | tf_op jit(solution)/shard_map/ppermute | solution.py:24
  16.4 6.8 %copy-start.2 = (f32[128,512]{1,0:T(8,128)S(1)}, f32[128,512]{1,0:T(8,128)}, u32[]{:S(2)}) copy-start(f32[128,512]{1,0:T(8,128)} %param.8) | copy-start | bytes 786436
  16.4 6.8 %copy-start.3 = (f32[128,512]{1,0:T(8,128)S(1)}, f32[128,512]{1,0:T(8,128)}, u32[]{:S(2)}) copy-start(f32[128,512]{1,0:T(8,128)} %param.9) | copy-start | bytes 786436
  26.1 6.9 %collective-permute-start.6 = (bf16[128,512]{1,0:T(8,128)(2,1)S(1)}, bf16[128,512]{1,0:T(8,128)(2,1)S(1)}, u32[]{:S(2)}, u32[]{:S(2)}) collective-permute-start(bf16[128,512]{1,0:T(8,128)(2,1)S(1)} %get-tuple-element.4), channel_id=1, source_target_pairs={{0,24},{4,28},{8,16},{12,20},{16,8},{20,12},{24,0},{28,4},{1,25},{... | collective-permute-start | bytes 393224 | tf_op jit(solution)/shard_map/ppermute | solution.py:24
  27.5 6.8 %collective-permute-start.5 = (bf16[128,512]{1,0:T(8,128)(2,1)S(1)}, bf16[128,512]{1,0:T(8,128)(2,1)S(1)}, u32[]{:S(2)}, u32[]{:S(2)}) collective-permute-start(bf16[128,512]{1,0:T(8,128)(2,1)S(1)} %get-tuple-element.4), channel_id=1, source_target_pairs={{0,16},{4,20},{8,24},{12,28},{16,0},{20,4},{24,8},{28,12},{1,17},{... | collective-permute-start | bytes 393224 | tf_op jit(solution)/shard_map/ppermute | solution.py:24
  29.1 5.3 %collective-permute-start.4 = (bf16[128,512]{1,0:T(8,128)(2,1)S(1)}, bf16[128,512]{1,0:T(8,128)(2,1)S(1)}, u32[]{:S(2)}, u32[]{:S(2)}) collective-permute-start(bf16[128,512]{1,0:T(8,128)(2,1)S(1)} %get-tuple-element.4), channel_id=1, source_target_pairs={{0,8},{4,12},{8,0},{12,4},{16,24},{20,28},{24,16},{28,20},{1,9},{5... | collective-permute-start | bytes 393224 | tf_op jit(solution)/shard_map/ppermute | solution.py:24
  34.4 2.7 %collective-permute-start.7 = (bf16[4,128,512]{2,1,0:T(8,128)(2,1)S(1)}, bf16[4,128,512]{2,1,0:T(8,128)(2,1)S(1)}, u32[]{:S(2)}, u32[]{:S(2)}) collective-permute-start(bf16[4,128,512]{2,1,0:T(8,128)(2,1)S(1)} %pad_maximum_fusion.1), channel_id=1, source_target_pairs={{0,4},{4,0},{8,12},{12,8},{16,20},{20,16},{24,28},{28,24},{1,5},{5... | collective-permute-start | bytes 1572872 | tf_op jit(solution)/shard_map/ppermute | solution.py:27
  37.2 1.0 %copy-start.1 = (bf16[128,4096]{1,0:T(8,128)(2,1)}, bf16[128,4096]{1,0:T(8,128)(2,1)S(1)}, u32[]{:S(2)}) copy-start(bf16[128,4096]{1,0:T(8,128)(2,1)S(1)} %fusion.6) | copy-start | bytes 3145732

commit v2 on v1

v2 whole, which is shorter than its diff:
```python
import jax
import jax.numpy as jnp
from jax import lax
from jax.experimental import pallas as pl
from jax.experimental.pallas import tpu as pltpu
from jax.sharding import PartitionSpec as P

SMEM = pl.BlockSpec(memory_space=pltpu.SMEM)
VMEM = pl.BlockSpec(memory_space=pltpu.VMEM)
ANY = pl.BlockSpec(memory_space=pl.ANY)


def vmem(x):
    return pltpu.with_memory_space_constraint(x, pltpu.VMEM)


def shards(deltas, presence, owner_of, outer_params, momentum):
    groups = lax.axis_size("rep")
    pair = 2 if groups % 2 == 0 else 1
    chips = groups // pair
    flips = chips & (chips - 1) == 0
    rows = deltas.shape[1]
    width = deltas.shape[2] // groups
    bf16, f32 = jnp.bfloat16, jnp.float32

    def target(at, step):
        return at ^ step if flips else (at + step) % chips

    def origin(at, step):
        return at ^ step if flips else (at - step) % chips

    def across(x, step):
        return lax.ppermute(x, "rep", [(i, target(i // pair, step) * pair + i % pair) for i in range(groups)])

    def partner(x):
        return lax.ppermute(x, "rep", [(i, i ^ 1) for i in range(groups)])

    def where():
        me = lax.axis_index("rep")
        return me // pair, me % pair

    def columns(owner, ref, at):
        return ref.at[:, pl.ds(pl.multiple_of(owner[at] * width, width), width)]

    def load(owner, delta, *refs):
        outs, sem = refs[:-1], refs[-1]
        chip, core = where()
        copies = []
        for side, out in enumerate(outs):
            for s in range(chips):
                at = target(chip, s) * pair + (core + side) % pair
                copies.append(pltpu.make_async_copy(columns(owner, delta.at[0], at), out.at[s], sem.at[side, s]))
        for copy in reversed(copies):
            copy.start()
        for copy in copies:
            copy.wait()

    blocks = jax.ShapeDtypeStruct((chips, rows, width), bf16)
    held = pl.pallas_call(
        load,
        in_specs=[SMEM, ANY],
        out_specs=[VMEM] * pair,
        out_shape=[pltpu.VMEM((chips, rows, width), bf16)] * pair,
        scratch_shapes=[pltpu.SemaphoreType.DMA((pair, chips))],
        name="load",
    )(owner_of, deltas)
    arrived = [held[0]] + [partner(x) for x in held[1:]]

    def pair_sum(flag, *refs):
        ins, outs = refs[:pair], refs[pair:]
        me = lax.axis_index("rep")
        flags = [flag[me].astype(f32), flag[me ^ 1].astype(f32)][:pair]
        for s in range(chips):
            value = sum(x[s].astype(f32) * p for x, p in zip(ins, flags))
            outs[s][...] = value.astype(outs[s].dtype)

    sums = pl.pallas_call(
        pair_sum,
        in_specs=[SMEM] + [VMEM] * pair,
        out_specs=[VMEM] * chips,
        out_shape=[pltpu.VMEM((rows, width), bf16 if s else f32) for s in range(chips)],
        name="pair_sum",
    )(presence, *[vmem(x) for x in arrived])
    total = sums[0]
    for s in range(1, chips):
        total = total + across(sums[s], s).astype(f32)
    count = jnp.sum(presence.astype(f32))
    average = total / count
    new_momentum = 0.9 * momentum + average
    new_outer = outer_params - 0.7 * (average + 0.9 * new_momentum)
    shipped = new_outer.astype(bf16)
    got = jnp.stack([shipped] + [across(shipped, s) for s in range(1, chips)])
    parts = [got] + [partner(got)] * (pair - 1)

    def place(owner, *refs):
        ins, out, sem = refs[:pair], refs[pair], refs[pair + 1]
        chip, core = where()
        copies = []
        for side, x in enumerate(ins):
            for s in range(chips):
                at = origin(chip, s) * pair + (core + side) % pair
                copies.append(pltpu.make_async_copy(x.at[s], columns(owner, out, at), sem.at[side, s]))
        for copy in copies:
            copy.start()
        for copy in copies:
            copy.wait()

    new_weights = pl.pallas_call(
        place,
        in_specs=[SMEM] + [VMEM] * pair,
        out_specs=ANY,
        out_shape=jax.ShapeDtypeStruct((rows, groups * width), bf16),
        scratch_shapes=[pltpu.SemaphoreType.DMA((pair, chips))],
        name="place",
    )(owner_of, *[vmem(x) for x in parts])
    return (new_weights, new_outer, new_momentum)


def solution(mesh):
    return jax.shard_map(
        shards,
        mesh=mesh,
        in_specs=(P("rep", "shard", None), P(), P(), P("shard", "rep"), P("shard", "rep")),
        out_specs=(P("shard", None), P("shard", "rep"), P("shard", "rep")),
        check_vma=False,
    )
```

time: 38.5 us -> 30.5 us (0.79)
  between operations: 8.49 us -> 0.67 us
  local copies, waits for them, and re-layouts: 5.02 us -> 0.01 us
  Pallas kernels: 0 us -> 4.77 us
  other arithmetic: 4.98 us -> 2.23 us
  waiting for transfers between devices: 11.5 us -> 14.1 us
    pallas_call x0 -> x3, Pallas kernels: none -> 4.77 us  [the longest x1 2.06 us: shards(): pl.pallas_call(load, in_specs=[SMEM, ANY], out_specs=[VMEM] * pair, out_s...]
    ppermute x2, waiting for transfers between devices: 0.01 us -> 3.43 us  [partner(): return lax.ppermute(x, 'rep', [(i, i ^ 1) for i in range(groups)])]
    dynamic_update_slice x1 -> x0, other arithmetic: 2.83 us -> none  [shards(): new_weights = lax.dynamic_update_slice(new_weights, held[s], (0, at))]
    dynamic_slice x3 -> x0, local copies, waits for them, and re-layouts: 2.54 us -> none  [the longest x1 1.23 us: block(): lax.dynamic_slice(deltas[0], (0, owner_of[index] * width), (rows, width))]
    unnamed x12 -> x6, local copies, waits for them, and re-layouts: 2.28 us -> 0.01 us
    ppermute x6, waiting for transfers between devices: 11.5 us -> 10.6 us  [across(): lax.ppermute(x, 'rep', [(i, target(i // pair, step) * pair + i % pair) fo...]
    convert_element_type x2 -> x1, other arithmetic: 1.34 us -> 1.57 us  [shards(): shipped = new_outer.astype(bf16)]
  transfers between devices with their start and end apart: 8 -> 8, of which waited for: 5 -> 7; matrix products, arithmetic and copies ran while one was open for 3% -> 2% of each run, Pallas kernels for 0% -> 0%
where the time goes in v2:
time: 30.5 us; the launch traced here: 30.3 us
  waiting for transfers between devices  14.1 us (46%)
  starting transfers between devices  8.58 us (28%)
  Pallas kernels  4.77 us (16%)
  other arithmetic  2.23 us (7%)
  between operations  0.67 us (2%)
    ppermute x6, waiting for transfers between devices, across(): lax.ppermute(x, 'rep', [(i, target(i // pair, step) * pair + i % pair) fo...  10.6 us
    ppermute x6, starting transfers between devices, across(): lax.ppermute(x, 'rep', [(i, target(i // pair, step) * pair + i % pair) fo...  7.95 us
    ppermute x2, waiting for transfers between devices, partner(): return lax.ppermute(x, 'rep', [(i, i ^ 1) for i in range(groups)])  3.43 us
    pallas_call x1, Pallas kernels, shards(): pl.pallas_call(load, in_specs=[SMEM, ANY], out_specs=[VMEM] * pair, out_s...  2.06 us
    pallas_call x1, Pallas kernels, shards(): pl.pallas_call(place, in_specs=[SMEM] + [VMEM] * pair, out_specs=ANY, out...  1.71 us
    convert_element_type x1, other arithmetic, shards(): shipped = new_outer.astype(bf16)  1.57 us
    pallas_call x1, Pallas kernels, shards(): pl.pallas_call(pair_sum, in_specs=[SMEM] + [VMEM] * pair, out_specs=[VMEM...  0.99 us
    ppermute x2, starting transfers between devices, partner(): return lax.ppermute(x, 'rep', [(i, i ^ 1) for i in range(groups)])  0.63 us
  transfers between devices with their start and end apart: 8, of which 7 were waited for; matrix products, arithmetic and copies ran while one was open for 2% of the time, Pallas kernels for 0%

profile of v2, /device:TPU:0, one launch (start us, length us, event | category | flops | bytes accessed | tf_op | source)
XLA Modules:
  0.0 30.3 jit_solution(12057182717942746523)
XLA Ops:
  0.6 2.1 %load.1 = (bf16[4,128,512]{2,1,0:T(8,128)(2,1)S(1)}, bf16[4,128,512]{2,1,0:T(8,128)(2,1)S(1)}) custom-call(s32[8]{0:T(128)} %owner.3, bf16[1,128,4096]{2,1,0:T(8,128)(2,1)} %delta.1), custom_call_target="tpu_custom_call" | custom-call | tf_op jit(solution)/shard_map/load/pallas_call | solution.py:59
  2.7 0.6 %collective-permute-start = (bf16[4,128,512]{2,1,0:T(8,128)(2,1)S(1)}, bf16[4,128,512]{2,1,0:T(8,128)(2,1)S(1)}, u32[]{:S(2)}, u32[]{:S(2)}) collective-permute-start(bf16[4,128,512]{2,1,0:T(8,128)(2,1)S(1)} %get-tuple-element.10), channel_id=1, source_target_pairs={{0,4},{4,0},{8,12},{12,8},{16,20},{20,16},{24,28},{28,24},{1,5},{5... | collective-permute-start | bytes 1572872 | tf_op jit(solution)/shard_map/ppermute | solution.py:36
  3.3 1.5 %collective-permute-done.refs_1_ = bf16[4,128,512]{2,1,0:T(8,128)(2,1)S(1)} collective-permute-done((bf16[4,128,512]{2,1,0:T(8,128)(2,1)S(1)}, bf16[4,128,512]{2,1,0:T(8,128)(2,1)S(1)}, u32[]{:S(2)}, u32[]{:S(2)}) %collective-permute-start) | collective-permute-done | bytes 524320 | tf_op jit(solution)/shard_map/ppermute | solution.py:36
  4.8 1.0 %pair_sum.1 = (f32[128,512]{1,0:T(8,128)S(1)}, bf16[128,512]{1,0:T(8,128)(2,1)S(1)}, bf16[128,512]{1,0:T(8,128)(2,1)S(1)}, bf16[128,512]{1,0:T(8,128)(2,1)S(1)}) custom-call(s32[8]{0:T(128)} %flag.1, bf16[4,128,512]{2,1,0:T(8,128)(2,1)S(1)} %get-tuple-element.9.refs_0_, bf16[4,128,512]{2,1,0:T(8,128)(2,1)S(1)} %collective-permute-done.refs_1_), custom_call_target="tpu_custom_call" | custom-call | tf_op jit(solution)/shard_map/pair_sum/pallas_call | solution.py:77
  5.8 2.9 %collective-permute-start.1 = (bf16[128,512]{1,0:T(8,128)(2,1)S(1)}, bf16[128,512]{1,0:T(8,128)(2,1)S(1)}, u32[]{:S(2)}, u32[]{:S(2)}) collective-permute-start(bf16[128,512]{1,0:T(8,128)(2,1)S(1)} %get-tuple-element.12), channel_id=1, source_target_pairs={{0,8},{4,12},{8,0},{12,4},{16,24},{20,28},{24,16},{28,20},{1,9},{5... | collective-permute-start | bytes 393224 | tf_op jit(solution)/shard_map/ppermute | solution.py:33
  8.7 1.5 %collective-permute-start.2 = (bf16[128,512]{1,0:T(8,128)(2,1)S(1)}, bf16[128,512]{1,0:T(8,128)(2,1)S(1)}, u32[]{:S(2)}, u32[]{:S(2)}) collective-permute-start(bf16[128,512]{1,0:T(8,128)(2,1)S(1)} %get-tuple-element.13), channel_id=1, source_target_pairs={{0,16},{4,20},{8,24},{12,28},{16,0},{20,4},{24,8},{28,12},{1,17},{... | collective-permute-start | bytes 393224 | tf_op jit(solution)/shard_map/ppermute | solution.py:33
  10.2 0.0 collective-permute-start.3
  10.3 0.0 copy-done.2
  10.3 0.6 %convert_reduce_fusion = f32[]{:T(128)} fusion(s32[8]{0:T(128)S(1)} %copy-done.2), kind=kLoop, calls=%fused_computation.4 | loop fusion | flops 15 | bytes 36 | tf_op jit(solution)/shard_map/reduce_sum | solution.py:87
  10.9 1.8 %collective-permute-done.1 = bf16[128,512]{1,0:T(8,128)(2,1)S(1)} collective-permute-done((bf16[128,512]{1,0:T(8,128)(2,1)S(1)}, bf16[128,512]{1,0:T(8,128)(2,1)S(1)}, u32[]{:S(2)}, u32[]{:S(2)}) %collective-permute-start.1) | collective-permute-done | bytes 131104 | tf_op jit(solution)/shard_map/ppermute | solution.py:33
  12.7 4.1 %collective-permute-done.2 = bf16[128,512]{1,0:T(8,128)(2,1)S(1)} collective-permute-done((bf16[128,512]{1,0:T(8,128)(2,1)S(1)}, bf16[128,512]{1,0:T(8,128)(2,1)S(1)}, u32[]{:S(2)}, u32[]{:S(2)}) %collective-permute-start.2) | collective-permute-done | bytes 131104 | tf_op jit(solution)/shard_map/ppermute | solution.py:33
  16.8 0.0 collective-permute-done.3
  16.8 0.0 copy-done
  16.8 1.6 %fusion = (bf16[128,512]{1,0:T(8,128)(2,1)S(1)}, f32[128,512]{1,0:T(8,128)}, f32[128,512]{1,0:T(8,128)}) fusion(f32[128,512]{1,0:T(8,128)S(1)} %copy-done, f32[]{:T(128)} %convert_reduce_fusion, bf16[128,512]{1,0:T(8,128)(2,1)S(1)} %collective-permute-done.3, bf16[128,512]{1,0:T(8,128)(2,1)S(1)} %collective-permute-done.2, ...), kind=kLoop, calls=%fused_computation.5 | loop fusion | flops 917504 | bytes 1835012 | tf_op jit(solution)/shard_map/convert_element_type | solution.py:91
  18.4 1.5 %collective-permute-start.6 = (bf16[128,512]{1,0:T(8,128)(2,1)S(1)}, bf16[128,512]{1,0:T(8,128)(2,1)S(1)}, u32[]{:S(2)}, u32[]{:S(2)}) collective-permute-start(bf16[128,512]{1,0:T(8,128)(2,1)S(1)} %get-tuple-element.15), channel_id=1, source_target_pairs={{0,24},{4,28},{8,16},{12,20},{16,8},{20,12},{24,0},{28,4},{1,25},{... | collective-permute-start | bytes 393224 | tf_op jit(solution)/shard_map/ppermute | solution.py:33
  19.9 1.2 %collective-permute-start.5 = (bf16[128,512]{1,0:T(8,128)(2,1)S(1)}, bf16[128,512]{1,0:T(8,128)(2,1)S(1)}, u32[]{:S(2)}, u32[]{:S(2)}) collective-permute-start(bf16[128,512]{1,0:T(8,128)(2,1)S(1)} %get-tuple-element.15), channel_id=1, source_target_pairs={{0,16},{4,20},{8,24},{12,28},{16,0},{20,4},{24,8},{28,12},{1,17},{... | collective-permute-start | bytes 393224 | tf_op jit(solution)/shard_map/ppermute | solution.py:33
  21.0 0.8 %collective-permute-start.4 = (bf16[128,512]{1,0:T(8,128)(2,1)S(1)}, bf16[128,512]{1,0:T(8,128)(2,1)S(1)}, u32[]{:S(2)}, u32[]{:S(2)}) collective-permute-start(bf16[128,512]{1,0:T(8,128)(2,1)S(1)} %get-tuple-element.15), channel_id=1, source_target_pairs={{0,8},{4,12},{8,0},{12,4},{16,24},{20,28},{24,16},{28,20},{1,9},{5... | collective-permute-start | bytes 393224 | tf_op jit(solution)/shard_map/ppermute | solution.py:33
  21.9 3.4 %collective-permute-done.6 = bf16[128,512]{1,0:T(8,128)(2,1)S(1)} collective-permute-done((bf16[128,512]{1,0:T(8,128)(2,1)S(1)}, bf16[128,512]{1,0:T(8,128)(2,1)S(1)}, u32[]{:S(2)}, u32[]{:S(2)}) %collective-permute-start.6) | collective-permute-done | bytes 131104 | tf_op jit(solution)/shard_map/ppermute | solution.py:33
  25.3 1.1 %collective-permute-done.5 = bf16[128,512]{1,0:T(8,128)(2,1)S(1)} collective-permute-done((bf16[128,512]{1,0:T(8,128)(2,1)S(1)}, bf16[128,512]{1,0:T(8,128)(2,1)S(1)}, u32[]{:S(2)}, u32[]{:S(2)}) %collective-permute-start.5) | collective-permute-done | bytes 131104 | tf_op jit(solution)/shard_map/ppermute | solution.py:33
  26.4 0.2 collective-permute-done.4
  26.6 0.1 pad_maximum_fusion.refs_0_
  26.6 0.1 collective-permute-start.7
  26.7 1.9 %collective-permute-done.7.refs_1_ = bf16[4,128,512]{2,1,0:T(8,128)(2,1)S(1)} collective-permute-done((bf16[4,128,512]{2,1,0:T(8,128)(2,1)S(1)}, bf16[4,128,512]{2,1,0:T(8,128)(2,1)S(1)}, u32[]{:S(2)}, u32[]{:S(2)}) %collective-permute-start.7) | collective-permute-done | bytes 524320 | tf_op jit(solution)/shard_map/ppermute | solution.py:36
  28.6 1.7 %place.1 = bf16[128,4096]{1,0:T(8,128)(2,1)} custom-call(s32[8]{0:T(128)} %owner.3, bf16[4,128,512]{2,1,0:T(8,128)(2,1)S(1)} %pad_maximum_fusion.refs_0_, bf16[4,128,512]{2,1,0:T(8,128)(2,1)S(1)} %collective-permute-done.7.refs_1_), custom_call_target="tpu_custom_call" | custom-call | tf_op jit(solution)/shard_map/place/pallas_call | solution.py:108
  (4 shorter events, 0.0 us)
Async XLA Ops:
  2.7 2.1 %collective-permute-start = (bf16[4,128,512]{2,1,0:T(8,128)(2,1)S(1)}, bf16[4,128,512]{2,1,0:T(8,128)(2,1)S(1)}, u32[]{:S(2)}, u32[]{:S(2)}) collective-permute-start(bf16[4,128,512]{2,1,0:T(8,128)(2,1)S(1)} %get-tuple-element.10), channel_id=1, source_target_pairs={{0,4},{4,0},{8,12},{12,8},{16,20},{20,16},{24,28},{28,24},{1,5},{5... | collective-permute-start | bytes 1572872 | tf_op jit(solution)/shard_map/ppermute | solution.py:36
  4.8 12.0 %copy-start = (f32[128,512]{1,0:T(8,128)S(1)}, f32[128,512]{1,0:T(8,128)}, u32[]{:S(2)}) copy-start(f32[128,512]{1,0:T(8,128)} %param.8) | copy-start | bytes 786436
  4.8 12.0 %copy-start.1 = (f32[128,512]{1,0:T(8,128)S(1)}, f32[128,512]{1,0:T(8,128)}, u32[]{:S(2)}) copy-start(f32[128,512]{1,0:T(8,128)} %param.9) | copy-start | bytes 786436
  5.8 6.9 %collective-permute-start.1 = (bf16[128,512]{1,0:T(8,128)(2,1)S(1)}, bf16[128,512]{1,0:T(8,128)(2,1)S(1)}, u32[]{:S(2)}, u32[]{:S(2)}) collective-permute-start(bf16[128,512]{1,0:T(8,128)(2,1)S(1)} %get-tuple-element.12), channel_id=1, source_target_pairs={{0,8},{4,12},{8,0},{12,4},{16,24},{20,28},{24,16},{28,20},{1,9},{5... | collective-permute-start | bytes 393224 | tf_op jit(solution)/shard_map/ppermute | solution.py:33
  8.7 1.6 %copy-start.2 = (s32[8]{0:T(128)S(1)}, s32[8]{0:T(128)}, u32[]{:S(2)}) copy-start(s32[8]{0:T(128)} %flag.1) | copy-start | bytes 100
  8.7 8.1 %collective-permute-start.2 = (bf16[128,512]{1,0:T(8,128)(2,1)S(1)}, bf16[128,512]{1,0:T(8,128)(2,1)S(1)}, u32[]{:S(2)}, u32[]{:S(2)}) collective-permute-start(bf16[128,512]{1,0:T(8,128)(2,1)S(1)} %get-tuple-element.13), channel_id=1, source_target_pairs={{0,16},{4,20},{8,24},{12,28},{16,0},{20,4},{24,8},{28,12},{1,17},{... | collective-permute-start | bytes 393224 | tf_op jit(solution)/shard_map/ppermute | solution.py:33
  10.2 6.6 %collective-permute-start.3 = (bf16[128,512]{1,0:T(8,128)(2,1)S(1)}, bf16[128,512]{1,0:T(8,128)(2,1)S(1)}, u32[]{:S(2)}, u32[]{:S(2)}) collective-permute-start(bf16[128,512]{1,0:T(8,128)(2,1)S(1)} %get-tuple-element.14), channel_id=1, source_target_pairs={{0,24},{4,28},{8,16},{12,20},{16,8},{20,12},{24,0},{28,4},{1,25},{... | collective-permute-start | bytes 393224 | tf_op jit(solution)/shard_map/ppermute | solution.py:33
  18.4 6.9 %collective-permute-start.6 = (bf16[128,512]{1,0:T(8,128)(2,1)S(1)}, bf16[128,512]{1,0:T(8,128)(2,1)S(1)}, u32[]{:S(2)}, u32[]{:S(2)}) collective-permute-start(bf16[128,512]{1,0:T(8,128)(2,1)S(1)} %get-tuple-element.15), channel_id=1, source_target_pairs={{0,24},{4,28},{8,16},{12,20},{16,8},{20,12},{24,0},{28,4},{1,25},{... | collective-permute-start | bytes 393224 | tf_op jit(solution)/shard_map/ppermute | solution.py:33
  19.9 6.5 %collective-permute-start.5 = (bf16[128,512]{1,0:T(8,128)(2,1)S(1)}, bf16[128,512]{1,0:T(8,128)(2,1)S(1)}, u32[]{:S(2)}, u32[]{:S(2)}) collective-permute-start(bf16[128,512]{1,0:T(8,128)(2,1)S(1)} %get-tuple-element.15), channel_id=1, source_target_pairs={{0,16},{4,20},{8,24},{12,28},{16,0},{20,4},{24,8},{28,12},{1,17},{... | collective-permute-start | bytes 393224 | tf_op jit(solution)/shard_map/ppermute | solution.py:33
  21.0 5.5 %collective-permute-start.4 = (bf16[128,512]{1,0:T(8,128)(2,1)S(1)}, bf16[128,512]{1,0:T(8,128)(2,1)S(1)}, u32[]{:S(2)}, u32[]{:S(2)}) collective-permute-start(bf16[128,512]{1,0:T(8,128)(2,1)S(1)} %get-tuple-element.15), channel_id=1, source_target_pairs={{0,8},{4,12},{8,0},{12,4},{16,24},{20,28},{24,16},{28,20},{1,9},{5... | collective-permute-start | bytes 393224 | tf_op jit(solution)/shard_map/ppermute | solution.py:33
  26.6 2.0 %collective-permute-start.7 = (bf16[4,128,512]{2,1,0:T(8,128)(2,1)S(1)}, bf16[4,128,512]{2,1,0:T(8,128)(2,1)S(1)}, u32[]{:S(2)}, u32[]{:S(2)}) collective-permute-start(bf16[4,128,512]{2,1,0:T(8,128)(2,1)S(1)} %pad_maximum_fusion.refs_0_), channel_id=1, source_target_pairs={{0,4},{4,0},{8,12},{12,8},{16,20},{20,16},{24,28},{28,24},{1,5},{5... | collective-permute-start | bytes 1572872 | tf_op jit(solution)/shard_map/ppermute | solution.py:36

commit v3 on v0

v3 whole, which is shorter than its diff:
```python
import jax
import jax.numpy as jnp
from jax import lax
from jax.experimental import pallas as pl
from jax.experimental.pallas import tpu as pltpu
from jax.sharding import PartitionSpec as P


SMEM = pl.BlockSpec(memory_space=pltpu.SMEM)
VMEM = pl.BlockSpec(memory_space=pltpu.VMEM)
ANY = pl.BlockSpec(memory_space=pl.ANY)
HBM = pl.BlockSpec(memory_space=pltpu.HBM)


def vmem(x):
    return pltpu.with_memory_space_constraint(x, pltpu.VMEM)


def smem(x):
    return pltpu.with_memory_space_constraint(x, pltpu.SMEM)


def shards(deltas, presence, owner_of, outer_params, momentum):
    groups = lax.axis_size("rep")
    chips = groups // 2
    rows = deltas.shape[1]
    width = deltas.shape[2] // groups
    bf16, f32 = jnp.bfloat16, jnp.float32
    flips = sorted(range(chips), key=lambda m: (m.bit_count(), m))

    def direct(x, s):
        return lax.ppermute(x, "rep", [(i, i ^ 2 * flips[s]) for i in range(groups)])

    def swap(x):
        return lax.ppermute(x, "rep", [(i, i ^ 1) for i in range(groups)])

    def where():
        me = lax.axis_index("rep")
        return me // 2, me % 2

    def device(chip, core, s):
        return (chip ^ flips[s]) * 2 + core

    def columns(owner, at):
        return pl.ds(pl.multiple_of(owner[at] * width, width), width)

    def own_flag(flag):
        return flag[lax.axis_index("rep")].astype(f32)

    def tile(*lead, dtype=bf16):
        return pltpu.VMEM((*lead, rows, width), dtype)

    later = [*range(2, chips), 0]

    def load(owner_hbm, flag_hbm, delta, owner, flag, whole, head, tail, sem):
        copies = [
            pltpu.make_async_copy(delta.at[0], whole, sem.at[0]),
            pltpu.make_async_copy(owner_hbm, owner, sem.at[1]),
            pltpu.make_async_copy(flag_hbm, flag, sem.at[2]),
        ]
        for copy in copies:
            copy.start()
        for copy in reversed(copies):
            copy.wait()
        chip, core = where()
        own = own_flag(flag)

        def masked(s):
            return (whole[:, columns(owner, device(chip, 1 - core, s))].astype(f32) * own).astype(bf16)

        head[...] = masked(1)
        for i, s in enumerate(later):
            tail[i] = masked(s)

    owner_of, presence, whole, head, tail = pl.pallas_call(
        load,
        in_specs=[ANY] * 3,
        out_specs=[SMEM] * 2 + [VMEM] * 3,
        out_shape=[pltpu.SMEM((groups,), jnp.int32)] * 2
        + [pltpu.VMEM((rows, groups * width), bf16), tile(), tile(chips - 1)],
        scratch_shapes=[pltpu.SemaphoreType.DMA((3,))],
        name="load",
    )(owner_of, presence, deltas)
    owner_of, presence, whole = smem(owner_of), smem(presence), vmem(whole)
    head = swap(head)
    tail = swap(tail)

    def add(owner, flag, whole, got, s):
        chip, core = where()
        mine = whole[:, columns(owner, device(chip, core, s))].astype(f32)
        return mine * own_flag(flag) + got.astype(f32)

    def sum_head(owner, flag, whole, got, out):
        out[...] = add(owner, flag, whole, got[...], 1).astype(bf16)

    def sum_tail(owner, flag, whole, got, *outs):
        for i, s in enumerate(later):
            outs[i][...] = add(owner, flag, whole, got[i], s).astype(outs[i].dtype)

    head = pl.pallas_call(
        sum_head,
        in_specs=[SMEM] * 2 + [VMEM] * 2,
        out_specs=VMEM,
        out_shape=tile(),
        name="sum_head",
    )(owner_of, presence, whole, vmem(head))
    terms = [direct(head, 1)]
    *sums, own_sum = pl.pallas_call(
        sum_tail,
        in_specs=[SMEM] * 2 + [VMEM] * 2,
        out_specs=[VMEM] * (chips - 1),
        out_shape=[tile()] * (chips - 2) + [tile(dtype=f32)],
        name="sum_tail",
    )(owner_of, presence, whole, vmem(tail))
    for s, x in enumerate(sums, 2):
        terms.append(direct(x, s))

    def update(flag, outer, velocity, *refs):
        ins, (ship, next_outer, next_velocity) = refs[:chips], refs[chips:]
        count = sum(flag[r] for r in range(groups)).astype(f32)
        average = sum(x[...].astype(f32) for x in ins) / count
        moved = 0.9 * velocity[...] + average
        stepped = outer[...] - 0.7 * (average + 0.9 * moved)
        next_velocity[...] = moved
        next_outer[...] = stepped
        ship[...] = stepped.astype(bf16)

    shipped, new_outer, new_momentum = pl.pallas_call(
        update,
        in_specs=[SMEM] + [VMEM] * (2 + chips),
        out_specs=[VMEM] * 3,
        out_shape=[tile(), tile(dtype=f32), tile(dtype=f32)],
        name="update",
    )(presence, *map(vmem, [outer_params, momentum, own_sum, *terms]))

    got = [shipped]
    for s in range(1, chips):
        got.append(direct(shipped, s))
    other = [swap(shipped)]
    for s in range(1, chips):
        other.append(swap(got[s]))

    def store(plan, into, extra=()):
        arrays = [x for x, *_ in plan]
        kept_in = [] if into is None else [into]

        def body(owner, *refs):
            ins = refs[: len(arrays)]
            wholes = refs[len(arrays) : len(arrays) + len(extra)]
            out, *outs = refs[len(arrays) + len(extra) + len(kept_in) : -1]
            sem = refs[-1]
            chip, core = where()
            pieces = list(zip(wholes, outs))
            for x, (_, side, s) in zip(ins, plan):
                at = device(chip, 1 - core if side else core, s)
                pieces.append((x, out.at[:, columns(owner, at)]))
            copies = [pltpu.make_async_copy(a, b, sem.at[i]) for i, (a, b) in enumerate(pieces)]
            for copy in copies:
                copy.start()
            for copy in copies:
                copy.wait()

        return pl.pallas_call(
            body,
            in_specs=[SMEM] + [VMEM] * (len(arrays) + len(extra)) + [HBM] * len(kept_in),
            out_specs=[HBM] * (1 + len(extra)),
            out_shape=[pltpu.HBM((rows, groups * width), bf16)] + [pltpu.HBM((rows, width), f32)] * len(extra),
            scratch_shapes=[pltpu.SemaphoreType.DMA((len(arrays) + len(extra),))],
            input_output_aliases={1 + len(arrays): 0} if kept_in else {},
            name="store",
        )(owner_of, *map(vmem, [*arrays, *extra]), *kept_in)

    tail = chips - 1
    new_weights, new_outer, new_momentum = store([(shipped, False, 0)], None, (new_outer, new_momentum))
    for s in range(1, tail + 1):
        plan = [(got[s], False, s)] + [(other[k], True, k) for k in range(max(s - 2, 0), s - 1)]
        if s == tail:
            plan += [(other[k], True, k) for k in (tail - 1, tail)]
        (new_weights,) = store(plan, new_weights)
    return (new_weights, new_outer, new_momentum)


def solution(mesh):
    return jax.shard_map(
        shards,
        mesh=mesh,
        in_specs=(P("rep", "shard", None), P(), P(), P("shard", "rep"), P("shard", "rep")),
        out_specs=(P("shard", None), P("shard", "rep"), P("shard", "rep")),
        check_vma=False,
    )
```

time: 91 us -> 27.6 us (0.30)
  waiting for transfers between devices: 58 us -> 12.7 us
  between operations: 14.2 us -> 0.74 us
  local copies, waits for them, and re-layouts: 11.5 us -> 0.01 us
  starting transfers between devices: 0.08 us -> 9.2 us
  other arithmetic: 6.97 us -> 0 us
  Pallas kernels: 0 us -> 4.78 us
    reduce_scatter x1 -> x0, waiting for transfers between devices: 37.1 us -> none  [shards(): lax.psum_scatter(term.astype(jnp.bfloat16), 'rep', scatter_dimension=1, t...]
    all_gather x1 -> x0, waiting for transfers between devices: 20.9 us -> none  [shards(): gathered = lax.all_gather(shipped, 'rep', axis=1, tiled=True)]
    ppermute x0 -> x12, waiting for transfers between devices: none -> 12.7 us  [the longest x6 11.2 us: direct(): lax.ppermute(x, 'rep', [(i, i ^ 2 * flips[s]) for i in range(groups)])]
    ppermute x0 -> x12, starting transfers between devices: none -> 9.2 us  [the longest x6 8.1 us: direct(): lax.ppermute(x, 'rep', [(i, i ^ 2 * flips[s]) for i in range(groups)])]
    unnamed x14 -> x4, local copies, waits for them, and re-layouts: 5.72 us -> 0.01 us
    pallas_call x0 -> x8, Pallas kernels: none -> 4.78 us  [the longest x4 3.13 us: store(): pl.pallas_call(body, in_specs=[SMEM] + [VMEM] * (len(arrays) + len(extra)...]
    convert_element_type x3 -> x0, other arithmetic: 3.9 us -> none  [the longest x1 2.29 us: shards(): shipped = new_outer.astype(jnp.bfloat16)]
    reshape x1 -> x0, local copies, waits for them, and re-layouts: 1.48 us -> none  [shards(): natural = jnp.take(gathered.reshape(rows, groups, width), inverse, axis=1)]
  transfers between devices with their start and end apart: 2 -> 12, of which waited for: 2 -> 6; matrix products, arithmetic and copies ran while one was open for 4% -> 0% of each run, Pallas kernels for 0% -> 9%
where the time goes in v3:
time: 27.6 us; the launch traced here: 27.4 us
  waiting for transfers between devices  12.7 us (46%)
  starting transfers between devices  9.2 us (33%)
  Pallas kernels  4.78 us (17%)
  between operations  0.74 us (3%)
    ppermute x6, waiting for transfers between devices, direct(): lax.ppermute(x, 'rep', [(i, i ^ 2 * flips[s]) for i in range(groups)])  11.2 us
    ppermute x6, starting transfers between devices, direct(): lax.ppermute(x, 'rep', [(i, i ^ 2 * flips[s]) for i in range(groups)])  8.1 us
    pallas_call x4, Pallas kernels, store(): pl.pallas_call(body, in_specs=[SMEM] + [VMEM] * (len(arrays) + len(extra)...  3.13 us
    ppermute x6, waiting for transfers between devices, swap(): return lax.ppermute(x, 'rep', [(i, i ^ 1) for i in range(groups)])  1.47 us
    pallas_call x1, Pallas kernels, shards(): pl.pallas_call(load, in_specs=[ANY] * 3, out_specs=[SMEM] * 2 + [VMEM] *...  1.34 us
    ppermute x6, starting transfers between devices, swap(): return lax.ppermute(x, 'rep', [(i, i ^ 1) for i in range(groups)])  1.1 us
  transfers between devices with their start and end apart: 12, of which 6 were waited for; matrix products, arithmetic and copies ran while one was open for 0% of the time, Pallas kernels for 9%

profile of v3, /device:TPU:0, one launch (start us, length us, event | category | flops | bytes accessed | tf_op | source)
XLA Modules:
  0.0 27.4 jit_solution(14148136576561234516)
XLA Ops:
  0.6 1.3 %load.1 = (s32[8]{0:T(128)S(4)}, s32[8]{0:T(128)S(4)}, bf16[128,4096]{1,0:T(8,128)(2,1)S(1)}, bf16[128,512]{1,0:T(8,128)(2,1)S(1)}, bf16[3,128,512]{2,1,0:T(8,128)(2,1)S(1)}) custom-call(s32[8]{0:T(128)} %owner_hbm.1, s32[8]{0:T(128)} %flag_hbm.1, bf16[1,128,4096]{2,1,0:T(8,128)(2,1)} %delta.1), custom_call_target="tpu_custom_call" | custom-call | tf_op jit(solution)/shard_map/load/pallas_call | solution.py:75
  2.0 0.6 %collective-permute-start = (bf16[3,128,512]{2,1,0:T(8,128)(2,1)S(1)}, bf16[3,128,512]{2,1,0:T(8,128)(2,1)S(1)}, u32[]{:S(2)}, u32[]{:S(2)}) collective-permute-start(bf16[3,128,512]{2,1,0:T(8,128)(2,1)S(1)} %get-tuple-element.20), channel_id=1, source_target_pairs={{0,4},{4,0},{8,12},{12,8},{16,20},{20,16},{24,28},{28,24},{1,5},{5... | collective-permute-start | bytes 1179656 | tf_op jit(solution)/shard_map/ppermute | solution.py:35
  2.5 0.1 collective-permute-start.1
  2.6 1.5 %collective-permute-done.1.got = bf16[128,512]{1,0:T(8,128)(2,1)S(1)} collective-permute-done((bf16[128,512]{1,0:T(8,128)(2,1)S(1)}, bf16[128,512]{1,0:T(8,128)(2,1)S(1)}, u32[]{:S(2)}, u32[]{:S(2)}) %collective-permute-start.1) | collective-permute-done | bytes 131104 | tf_op jit(solution)/shard_map/ppermute | solution.py:35
  4.1 0.0 copy-start
  4.1 0.0 copy-start.1
  4.1 2.9 %collective-permute-start.2 = (bf16[128,512]{1,0:T(8,128)(2,1)S(1)}, bf16[128,512]{1,0:T(8,128)(2,1)S(1)}, u32[]{:S(2)}, u32[]{:S(2)}) collective-permute-start(bf16[128,512]{1,0:T(8,128)(2,1)S(1)} %sum_head.1), channel_id=1, source_target_pairs={{0,8},{4,12},{8,0},{12,4},{16,24},{20,28},{24,16},{28,20},{1,9},{5... | collective-permute-start | bytes 393224 | tf_op jit(solution)/shard_map/ppermute | solution.py:32
  7.1 0.1 sum_tail.1
  7.2 1.6 %collective-permute-start.3 = (bf16[128,512]{1,0:T(8,128)(2,1)S(1)}, bf16[128,512]{1,0:T(8,128)(2,1)S(1)}, u32[]{:S(2)}, u32[]{:S(2)}) collective-permute-start(bf16[128,512]{1,0:T(8,128)(2,1)S(1)} %get-tuple-element.23), channel_id=1, source_target_pairs={{0,16},{4,20},{8,24},{12,28},{16,0},{20,4},{24,8},{28,12},{1,17},{... | collective-permute-start | bytes 393224 | tf_op jit(solution)/shard_map/ppermute | solution.py:32
  8.8 0.0 collective-permute-start.4
  8.8 2.1 %collective-permute-done.2.refs_1_ = bf16[128,512]{1,0:T(8,128)(2,1)S(1)} collective-permute-done((bf16[128,512]{1,0:T(8,128)(2,1)S(1)}, bf16[128,512]{1,0:T(8,128)(2,1)S(1)}, u32[]{:S(2)}, u32[]{:S(2)}) %collective-permute-start.2) | collective-permute-done | bytes 131104 | tf_op jit(solution)/shard_map/ppermute | solution.py:32
  10.9 4.4 %collective-permute-done.3.refs_2_ = bf16[128,512]{1,0:T(8,128)(2,1)S(1)} collective-permute-done((bf16[128,512]{1,0:T(8,128)(2,1)S(1)}, bf16[128,512]{1,0:T(8,128)(2,1)S(1)}, u32[]{:S(2)}, u32[]{:S(2)}) %collective-permute-start.3) | collective-permute-done | bytes 131104 | tf_op jit(solution)/shard_map/ppermute | solution.py:32
  15.3 0.1 update.1
  15.5 1.6 %collective-permute-start.5 = (bf16[128,512]{1,0:T(8,128)(2,1)S(1)}, bf16[128,512]{1,0:T(8,128)(2,1)S(1)}, u32[]{:S(2)}, u32[]{:S(2)}) collective-permute-start(bf16[128,512]{1,0:T(8,128)(2,1)S(1)} %get-tuple-element.25.refs_0_), channel_id=1, source_target_pairs={{0,24},{4,28},{8,16},{12,20},{16,8},{20,12},{24,0},{28,4},{1,25},{... | collective-permute-start | bytes 393224 | tf_op jit(solution)/shard_map/ppermute | solution.py:32
  17.0 1.5 %collective-permute-start.6 = (bf16[128,512]{1,0:T(8,128)(2,1)S(1)}, bf16[128,512]{1,0:T(8,128)(2,1)S(1)}, u32[]{:S(2)}, u32[]{:S(2)}) collective-permute-start(bf16[128,512]{1,0:T(8,128)(2,1)S(1)} %get-tuple-element.25.refs_0_), channel_id=1, source_target_pairs={{0,8},{4,12},{8,0},{12,4},{16,24},{20,28},{24,16},{28,20},{1,9},{5... | collective-permute-start | bytes 393224 | tf_op jit(solution)/shard_map/ppermute | solution.py:32
  18.5 0.5 %collective-permute-start.8 = (bf16[128,512]{1,0:T(8,128)(2,1)S(1)}, bf16[128,512]{1,0:T(8,128)(2,1)S(1)}, u32[]{:S(2)}, u32[]{:S(2)}) collective-permute-start(bf16[128,512]{1,0:T(8,128)(2,1)S(1)} %get-tuple-element.25.refs_0_), channel_id=1, source_target_pairs={{0,16},{4,20},{8,24},{12,28},{16,0},{20,4},{24,8},{28,12},{1,17},{... | collective-permute-start | bytes 393224 | tf_op jit(solution)/shard_map/ppermute | solution.py:32
  19.0 2.9 %collective-permute-done.5.refs_0_ = bf16[128,512]{1,0:T(8,128)(2,1)S(1)} collective-permute-done((bf16[128,512]{1,0:T(8,128)(2,1)S(1)}, bf16[128,512]{1,0:T(8,128)(2,1)S(1)}, u32[]{:S(2)}, u32[]{:S(2)}) %collective-permute-start.5) | collective-permute-done | bytes 131104 | tf_op jit(solution)/shard_map/ppermute | solution.py:32
  22.0 1.7 %collective-permute-done.6.refs_0_ = bf16[128,512]{1,0:T(8,128)(2,1)S(1)} collective-permute-done((bf16[128,512]{1,0:T(8,128)(2,1)S(1)}, bf16[128,512]{1,0:T(8,128)(2,1)S(1)}, u32[]{:S(2)}, u32[]{:S(2)}) %collective-permute-start.6) | collective-permute-done | bytes 131104 | tf_op jit(solution)/shard_map/ppermute | solution.py:32
  23.7 0.1 collective-permute-done.8.refs_0_
  23.8 0.5 %collective-permute-start.9 = (bf16[128,512]{1,0:T(8,128)(2,1)S(1)}, bf16[128,512]{1,0:T(8,128)(2,1)S(1)}, u32[]{:S(2)}, u32[]{:S(2)}) collective-permute-start(bf16[128,512]{1,0:T(8,128)(2,1)S(1)} %collective-permute-done.8.refs_0_), channel_id=1, source_target_pairs={{0,4},{4,0},{8,12},{12,8},{16,20},{20,16},{24,28},{28,24},{1,5},{5... | collective-permute-start | bytes 393224 | tf_op jit(solution)/shard_map/ppermute | solution.py:35
  24.2 0.9 %store.4 = (bf16[128,4096]{1,0:T(8,128)(2,1)}, f32[128,512]{1,0:T(8,128)}, f32[128,512]{1,0:T(8,128)}) custom-call(s32[8]{0:T(128)S(4)} %get-tuple-element.17.owner, bf16[128,512]{1,0:T(8,128)(2,1)S(1)} %get-tuple-element.25.refs_0_, f32[128,512]{1,0:T(8,128)S(1)} %get-tuple-element.26.refs_1_, f32[128,512]{1,0:T(8,128)S(1)} %get-tuple-element.27.refs_2_), custom_call_target="tpu_custom_call" | custom-call | tf_op jit(solution)/shard_map/store/pallas_call | solution.py:163
  25.1 0.7 %store.5.refs_2_ = bf16[128,4096]{1,0:T(8,128)(2,1)} custom-call(s32[8]{0:T(128)S(4)} %get-tuple-element.17.owner, bf16[128,512]{1,0:T(8,128)(2,1)S(1)} %collective-permute-done.6.refs_0_, bf16[128,4096]{1,0:T(8,128)(2,1)} %get-tuple-element.28.refs_1_), custom_call_target="tpu_custom_call", output_to_operand_aliasing={{}: (2, {})} | custom-call | tf_op jit(solution)/shard_map/store/pallas_call | solution.py:163
  25.8 0.7 %store.6.refs_4_ = bf16[128,4096]{1,0:T(8,128)(2,1)} custom-call(s32[8]{0:T(128)S(4)} %get-tuple-element.17.owner, bf16[128,512]{1,0:T(8,128)(2,1)S(1)} %collective-permute-done.8.refs_0_, bf16[128,512]{1,0:T(8,128)(2,1)S(1)} %collective-permute-done.11.refs_1_, bf16[128,4096]{1,0:T(8,128)(2,1)} %store.5.refs_2_), custom_call_target="tpu_custom_call", output_to_operand_aliasing={{}: (3, {})} | custom-call | tf_op jit(solution)/shard_map/store/pallas_call | solution.py:163
  26.6 0.8 %store.7 = bf16[128,4096]{1,0:T(8,128)(2,1)} custom-call(s32[8]{0:T(128)S(4)} %get-tuple-element.17.owner, bf16[128,512]{1,0:T(8,128)(2,1)S(1)} %collective-permute-done.5.refs_0_, bf16[128,512]{1,0:T(8,128)(2,1)S(1)} %collective-permute-done.7.refs_1_, bf16[128,512]{1,0:T(8,128)(2,1)S(1)} %collective-permute-done.9.refs_2_, ...), custom_call_target="tpu_custom_call", output_to_operand_aliasing={{}: (5, {})} | custom-call | tf_op jit(solution)/shard_map/store/pallas_call | solution.py:163
  (12 shorter events, 0.1 us)
Async XLA Ops:
  2.0 5.1 %collective-permute-start = (bf16[3,128,512]{2,1,0:T(8,128)(2,1)S(1)}, bf16[3,128,512]{2,1,0:T(8,128)(2,1)S(1)}, u32[]{:S(2)}, u32[]{:S(2)}) collective-permute-start(bf16[3,128,512]{2,1,0:T(8,128)(2,1)S(1)} %get-tuple-element.20), channel_id=1, source_target_pairs={{0,4},{4,0},{8,12},{12,8},{16,20},{20,16},{24,28},{28,24},{1,5},{5... | collective-permute-start | bytes 1179656 | tf_op jit(solution)/shard_map/ppermute | solution.py:35
  2.5 1.5 %collective-permute-start.1 = (bf16[128,512]{1,0:T(8,128)(2,1)S(1)}, bf16[128,512]{1,0:T(8,128)(2,1)S(1)}, u32[]{:S(2)}, u32[]{:S(2)}) collective-permute-start(bf16[128,512]{1,0:T(8,128)(2,1)S(1)} %get-tuple-element.22), channel_id=1, source_target_pairs={{0,4},{4,0},{8,12},{12,8},{16,20},{20,16},{24,28},{28,24},{1,5},{5... | collective-permute-start | bytes 393224 | tf_op jit(solution)/shard_map/ppermute | solution.py:35
  4.1 11.2 %copy-start = (f32[128,512]{1,0:T(8,128)S(1)}, f32[128,512]{1,0:T(8,128)}, u32[]{:S(2)}) copy-start(f32[128,512]{1,0:T(8,128)} %outer.1) | copy-start | bytes 786436
  4.1 11.2 %copy-start.1 = (f32[128,512]{1,0:T(8,128)S(1)}, f32[128,512]{1,0:T(8,128)}, u32[]{:S(2)}) copy-start(f32[128,512]{1,0:T(8,128)} %velocity.1) | copy-start | bytes 786436
  4.1 6.8 %collective-permute-start.2 = (bf16[128,512]{1,0:T(8,128)(2,1)S(1)}, bf16[128,512]{1,0:T(8,128)(2,1)S(1)}, u32[]{:S(2)}, u32[]{:S(2)}) collective-permute-start(bf16[128,512]{1,0:T(8,128)(2,1)S(1)} %sum_head.1), channel_id=1, source_target_pairs={{0,8},{4,12},{8,0},{12,4},{16,24},{20,28},{24,16},{28,20},{1,9},{5... | collective-permute-start | bytes 393224 | tf_op jit(solution)/shard_map/ppermute | solution.py:32
  7.2 8.1 %collective-permute-start.3 = (bf16[128,512]{1,0:T(8,128)(2,1)S(1)}, bf16[128,512]{1,0:T(8,128)(2,1)S(1)}, u32[]{:S(2)}, u32[]{:S(2)}) collective-permute-start(bf16[128,512]{1,0:T(8,128)(2,1)S(1)} %get-tuple-element.23), channel_id=1, source_target_pairs={{0,16},{4,20},{8,24},{12,28},{16,0},{20,4},{24,8},{28,12},{1,17},{... | collective-permute-start | bytes 393224 | tf_op jit(solution)/shard_map/ppermute | solution.py:32
  8.8 6.6 %collective-permute-start.4 = (bf16[128,512]{1,0:T(8,128)(2,1)S(1)}, bf16[128,512]{1,0:T(8,128)(2,1)S(1)}, u32[]{:S(2)}, u32[]{:S(2)}) collective-permute-start(bf16[128,512]{1,0:T(8,128)(2,1)S(1)} %get-tuple-element.24), channel_id=1, source_target_pairs={{0,24},{4,28},{8,16},{12,20},{16,8},{20,12},{24,0},{28,4},{1,25},{... | collective-permute-start | bytes 393224 | tf_op jit(solution)/shard_map/ppermute | solution.py:32
  15.5 6.5 %collective-permute-start.5 = (bf16[128,512]{1,0:T(8,128)(2,1)S(1)}, bf16[128,512]{1,0:T(8,128)(2,1)S(1)}, u32[]{:S(2)}, u32[]{:S(2)}) collective-permute-start(bf16[128,512]{1,0:T(8,128)(2,1)S(1)} %get-tuple-element.25.refs_0_), channel_id=1, source_target_pairs={{0,24},{4,28},{8,16},{12,20},{16,8},{20,12},{24,0},{28,4},{1,25},{... | collective-permute-start | bytes 393224 | tf_op jit(solution)/shard_map/ppermute | solution.py:32
  17.0 6.7 %collective-permute-start.6 = (bf16[128,512]{1,0:T(8,128)(2,1)S(1)}, bf16[128,512]{1,0:T(8,128)(2,1)S(1)}, u32[]{:S(2)}, u32[]{:S(2)}) collective-permute-start(bf16[128,512]{1,0:T(8,128)(2,1)S(1)} %get-tuple-element.25.refs_0_), channel_id=1, source_target_pairs={{0,8},{4,12},{8,0},{12,4},{16,24},{20,28},{24,16},{28,20},{1,9},{5... | collective-permute-start | bytes 393224 | tf_op jit(solution)/shard_map/ppermute | solution.py:32
  18.5 5.2 %collective-permute-start.8 = (bf16[128,512]{1,0:T(8,128)(2,1)S(1)}, bf16[128,512]{1,0:T(8,128)(2,1)S(1)}, u32[]{:S(2)}, u32[]{:S(2)}) collective-permute-start(bf16[128,512]{1,0:T(8,128)(2,1)S(1)} %get-tuple-element.25.refs_0_), channel_id=1, source_target_pairs={{0,16},{4,20},{8,24},{12,28},{16,0},{20,4},{24,8},{28,12},{1,17},{... | collective-permute-start | bytes 393224 | tf_op jit(solution)/shard_map/ppermute | solution.py:32
  19.0 6.7 %collective-permute-start.11 = (bf16[128,512]{1,0:T(8,128)(2,1)S(1)}, bf16[128,512]{1,0:T(8,128)(2,1)S(1)}, u32[]{:S(2)}, u32[]{:S(2)}) collective-permute-start(bf16[128,512]{1,0:T(8,128)(2,1)S(1)} %get-tuple-element.25.refs_0_), channel_id=1, source_target_pairs={{0,4},{4,0},{8,12},{12,8},{16,20},{20,16},{24,28},{28,24},{1,5},{5... | collective-permute-start | bytes 393224 | tf_op jit(solution)/shard_map/ppermute | solution.py:35
  22.0 4.6 %collective-permute-start.10 = (bf16[128,512]{1,0:T(8,128)(2,1)S(1)}, bf16[128,512]{1,0:T(8,128)(2,1)S(1)}, u32[]{:S(2)}, u32[]{:S(2)}) collective-permute-start(bf16[128,512]{1,0:T(8,128)(2,1)S(1)} %collective-permute-done.5.refs_0_), channel_id=1, source_target_pairs={{0,4},{4,0},{8,12},{12,8},{16,20},{20,16},{24,28},{28,24},{1,5},{5... | collective-permute-start | bytes 393224 | tf_op jit(solution)/shard_map/ppermute | solution.py:35
  23.7 2.8 %collective-permute-start.7 = (bf16[128,512]{1,0:T(8,128)(2,1)S(1)}, bf16[128,512]{1,0:T(8,128)(2,1)S(1)}, u32[]{:S(2)}, u32[]{:S(2)}) collective-permute-start(bf16[128,512]{1,0:T(8,128)(2,1)S(1)} %collective-permute-done.6.refs_0_), channel_id=1, source_target_pairs={{0,4},{4,0},{8,12},{12,8},{16,20},{20,16},{24,28},{28,24},{1,5},{5... | collective-permute-start | bytes 393224 | tf_op jit(solution)/shard_map/ppermute | solution.py:35
  23.8 2.8 %collective-permute-start.9 = (bf16[128,512]{1,0:T(8,128)(2,1)S(1)}, bf16[128,512]{1,0:T(8,128)(2,1)S(1)}, u32[]{:S(2)}, u32[]{:S(2)}) collective-permute-start(bf16[128,512]{1,0:T(8,128)(2,1)S(1)} %collective-permute-done.8.refs_0_), channel_id=1, source_target_pairs={{0,4},{4,0},{8,12},{12,8},{16,20},{20,16},{24,28},{28,24},{1,5},{5... | collective-permute-start | bytes 393224 | tf_op jit(solution)/shard_map/ppermute | solution.py:35

commit v4 on v3

--- a/solution.py
+++ b/solution.py
@@ -172,11 +172,12 @@
 
     tail = chips - 1
     new_weights, new_outer, new_momentum = store([(shipped, False, 0)], None, (new_outer, new_momentum))
-    for s in range(1, tail + 1):
-        plan = [(got[s], False, s)] + [(other[k], True, k) for k in range(max(s - 2, 0), s - 1)]
-        if s == tail:
-            plan += [(other[k], True, k) for k in (tail - 1, tail)]
+    for s in range(1, tail):
+        plan = [(got[s], False, s), *((other[k], True, k) for k in range(s - 1, s))]
+        if s == tail - 1:
+            plan += [(got[tail], False, tail), *((other[k], True, k) for k in range(tail - 1, tail))]
         (new_weights,) = store(plan, new_weights)
+    (new_weights,) = store([(other[tail], True, tail)], new_weights)
     return (new_weights, new_outer, new_momentum)
 
 

time: 27.6 us -> 27.2 us (0.986)
  starting transfers between devices: 9.2 us -> 8.75 us
    ppermute x6, starting transfers between devices: 1.1 us -> 0.65 us  [swap(): return lax.ppermute(x, 'rep', [(i, i ^ 1) for i in range(groups)])]
  transfers between devices with their start and end apart: 12 -> 12, of which waited for: 6 -> 6; matrix products, arithmetic and copies ran while one was open for 0% -> 0% of each run, Pallas kernels for 9% -> 10%
where the time goes in v4:
time: 27.2 us; the launch traced here: 27 us
  waiting for transfers between devices  12.8 us (47%)
  starting transfers between devices  8.75 us (32%)
  Pallas kernels  4.78 us (18%)
  between operations  0.74 us (3%)
    ppermute x6, waiting for transfers between devices, direct(): lax.ppermute(x, 'rep', [(i, i ^ 2 * flips[s]) for i in range(groups)])  11.3 us
    ppermute x6, starting transfers between devices, direct(): lax.ppermute(x, 'rep', [(i, i ^ 2 * flips[s]) for i in range(groups)])  8.1 us
    pallas_call x4, Pallas kernels, store(): pl.pallas_call(body, in_specs=[SMEM] + [VMEM] * (len(arrays) + len(extra)...  3.13 us
    ppermute x6, waiting for transfers between devices, swap(): return lax.ppermute(x, 'rep', [(i, i ^ 1) for i in range(groups)])  1.47 us
    pallas_call x1, Pallas kernels, shards(): pl.pallas_call(load, in_specs=[ANY] * 3, out_specs=[SMEM] * 2 + [VMEM] *...  1.34 us
    ppermute x6, starting transfers between devices, swap(): return lax.ppermute(x, 'rep', [(i, i ^ 1) for i in range(groups)])  0.65 us
  transfers between devices with their start and end apart: 12, of which 6 were waited for; matrix products, arithmetic and copies ran while one was open for 0% of the time, Pallas kernels for 10%

profile of v4, /device:TPU:0, one launch (start us, length us, event | category | flops | bytes accessed | tf_op | source)
XLA Modules:
  0.0 27.0 jit_solution(11599730138951507919)
XLA Ops:
  0.6 1.3 %load.1 = (s32[8]{0:T(128)S(4)}, s32[8]{0:T(128)S(4)}, bf16[128,4096]{1,0:T(8,128)(2,1)S(1)}, bf16[128,512]{1,0:T(8,128)(2,1)S(1)}, bf16[3,128,512]{2,1,0:T(8,128)(2,1)S(1)}) custom-call(s32[8]{0:T(128)} %owner_hbm.1, s32[8]{0:T(128)} %flag_hbm.1, bf16[1,128,4096]{2,1,0:T(8,128)(2,1)} %delta.1), custom_call_target="tpu_custom_call" | custom-call | tf_op jit(solution)/shard_map/load/pallas_call | solution.py:75
  2.0 0.6 %collective-permute-start = (bf16[3,128,512]{2,1,0:T(8,128)(2,1)S(1)}, bf16[3,128,512]{2,1,0:T(8,128)(2,1)S(1)}, u32[]{:S(2)}, u32[]{:S(2)}) collective-permute-start(bf16[3,128,512]{2,1,0:T(8,128)(2,1)S(1)} %get-tuple-element.20), channel_id=1, source_target_pairs={{0,4},{4,0},{8,12},{12,8},{16,20},{20,16},{24,28},{28,24},{1,5},{5... | collective-permute-start | bytes 1179656 | tf_op jit(solution)/shard_map/ppermute | solution.py:35
  2.5 0.1 collective-permute-start.1
  2.6 1.5 %collective-permute-done.1.got = bf16[128,512]{1,0:T(8,128)(2,1)S(1)} collective-permute-done((bf16[128,512]{1,0:T(8,128)(2,1)S(1)}, bf16[128,512]{1,0:T(8,128)(2,1)S(1)}, u32[]{:S(2)}, u32[]{:S(2)}) %collective-permute-start.1) | collective-permute-done | bytes 131104 | tf_op jit(solution)/shard_map/ppermute | solution.py:35
  4.1 0.0 copy-start
  4.1 0.0 copy-start.1
  4.1 2.9 %collective-permute-start.2 = (bf16[128,512]{1,0:T(8,128)(2,1)S(1)}, bf16[128,512]{1,0:T(8,128)(2,1)S(1)}, u32[]{:S(2)}, u32[]{:S(2)}) collective-permute-start(bf16[128,512]{1,0:T(8,128)(2,1)S(1)} %sum_head.1), channel_id=1, source_target_pairs={{0,8},{4,12},{8,0},{12,4},{16,24},{20,28},{24,16},{28,20},{1,9},{5... | collective-permute-start | bytes 393224 | tf_op jit(solution)/shard_map/ppermute | solution.py:32
  7.1 0.1 sum_tail.1
  7.2 1.6 %collective-permute-start.3 = (bf16[128,512]{1,0:T(8,128)(2,1)S(1)}, bf16[128,512]{1,0:T(8,128)(2,1)S(1)}, u32[]{:S(2)}, u32[]{:S(2)}) collective-permute-start(bf16[128,512]{1,0:T(8,128)(2,1)S(1)} %get-tuple-element.23), channel_id=1, source_target_pairs={{0,16},{4,20},{8,24},{12,28},{16,0},{20,4},{24,8},{28,12},{1,17},{... | collective-permute-start | bytes 393224 | tf_op jit(solution)/shard_map/ppermute | solution.py:32
  8.8 0.0 collective-permute-start.4
  8.8 2.1 %collective-permute-done.2.refs_1_ = bf16[128,512]{1,0:T(8,128)(2,1)S(1)} collective-permute-done((bf16[128,512]{1,0:T(8,128)(2,1)S(1)}, bf16[128,512]{1,0:T(8,128)(2,1)S(1)}, u32[]{:S(2)}, u32[]{:S(2)}) %collective-permute-start.2) | collective-permute-done | bytes 131104 | tf_op jit(solution)/shard_map/ppermute | solution.py:32
  10.9 4.4 %collective-permute-done.3.refs_2_ = bf16[128,512]{1,0:T(8,128)(2,1)S(1)} collective-permute-done((bf16[128,512]{1,0:T(8,128)(2,1)S(1)}, bf16[128,512]{1,0:T(8,128)(2,1)S(1)}, u32[]{:S(2)}, u32[]{:S(2)}) %collective-permute-start.3) | collective-permute-done | bytes 131104 | tf_op jit(solution)/shard_map/ppermute | solution.py:32
  15.3 0.0 collective-permute-done.4.refs_3_
  15.3 0.1 update.1
  15.5 1.6 %collective-permute-start.7 = (bf16[128,512]{1,0:T(8,128)(2,1)S(1)}, bf16[128,512]{1,0:T(8,128)(2,1)S(1)}, u32[]{:S(2)}, u32[]{:S(2)}) collective-permute-start(bf16[128,512]{1,0:T(8,128)(2,1)S(1)} %get-tuple-element.25.refs_0_), channel_id=1, source_target_pairs={{0,16},{4,20},{8,24},{12,28},{16,0},{20,4},{24,8},{28,12},{1,17},{... | collective-permute-start | bytes 393224 | tf_op jit(solution)/shard_map/ppermute | solution.py:32
  17.1 0.5 %collective-permute-start.8 = (bf16[128,512]{1,0:T(8,128)(2,1)S(1)}, bf16[128,512]{1,0:T(8,128)(2,1)S(1)}, u32[]{:S(2)}, u32[]{:S(2)}) collective-permute-start(bf16[128,512]{1,0:T(8,128)(2,1)S(1)} %get-tuple-element.25.refs_0_), channel_id=1, source_target_pairs={{0,8},{4,12},{8,0},{12,4},{16,24},{20,28},{24,16},{28,20},{1,9},{5... | collective-permute-start | bytes 393224 | tf_op jit(solution)/shard_map/ppermute | solution.py:32
  17.6 1.4 %collective-permute-start.5 = (bf16[128,512]{1,0:T(8,128)(2,1)S(1)}, bf16[128,512]{1,0:T(8,128)(2,1)S(1)}, u32[]{:S(2)}, u32[]{:S(2)}) collective-permute-start(bf16[128,512]{1,0:T(8,128)(2,1)S(1)} %get-tuple-element.25.refs_0_), channel_id=1, source_target_pairs={{0,24},{4,28},{8,16},{12,20},{16,8},{20,12},{24,0},{28,4},{1,25},{... | collective-permute-start | bytes 393224 | tf_op jit(solution)/shard_map/ppermute | solution.py:32
  19.0 2.9 %collective-permute-done.7.refs_0_ = bf16[128,512]{1,0:T(8,128)(2,1)S(1)} collective-permute-done((bf16[128,512]{1,0:T(8,128)(2,1)S(1)}, bf16[128,512]{1,0:T(8,128)(2,1)S(1)}, u32[]{:S(2)}, u32[]{:S(2)}) %collective-permute-start.7) | collective-permute-done | bytes 131104 | tf_op jit(solution)/shard_map/ppermute | solution.py:32
  21.9 0.7 %collective-permute-done.8.refs_0_ = bf16[128,512]{1,0:T(8,128)(2,1)S(1)} collective-permute-done((bf16[128,512]{1,0:T(8,128)(2,1)S(1)}, bf16[128,512]{1,0:T(8,128)(2,1)S(1)}, u32[]{:S(2)}, u32[]{:S(2)}) %collective-permute-start.8) | collective-permute-done | bytes 131104 | tf_op jit(solution)/shard_map/ppermute | solution.py:32
  22.6 1.2 %collective-permute-done.5.refs_2_ = bf16[128,512]{1,0:T(8,128)(2,1)S(1)} collective-permute-done((bf16[128,512]{1,0:T(8,128)(2,1)S(1)}, bf16[128,512]{1,0:T(8,128)(2,1)S(1)}, u32[]{:S(2)}, u32[]{:S(2)}) %collective-permute-start.5) | collective-permute-done | bytes 131104 | tf_op jit(solution)/shard_map/ppermute | solution.py:32
  23.8 0.9 %store.4 = (bf16[128,4096]{1,0:T(8,128)(2,1)}, f32[128,512]{1,0:T(8,128)}, f32[128,512]{1,0:T(8,128)}) custom-call(s32[8]{0:T(128)S(4)} %get-tuple-element.17.owner, bf16[128,512]{1,0:T(8,128)(2,1)S(1)} %get-tuple-element.25.refs_0_, f32[128,512]{1,0:T(8,128)S(1)} %get-tuple-element.26.refs_1_, f32[128,512]{1,0:T(8,128)S(1)} %get-tuple-element.27.refs_2_), custom_call_target="tpu_custom_call" | custom-call | tf_op jit(solution)/shard_map/store/pallas_call | solution.py:163
  24.7 0.7 %store.5.refs_4_ = bf16[128,4096]{1,0:T(8,128)(2,1)} custom-call(s32[8]{0:T(128)S(4)} %get-tuple-element.17.owner, bf16[128,512]{1,0:T(8,128)(2,1)S(1)} %collective-permute-done.8.refs_0_, bf16[128,512]{1,0:T(8,128)(2,1)S(1)} %collective-permute-done.11.refs_1_, bf16[128,4096]{1,0:T(8,128)(2,1)} %get-tuple-element.28.refs_2_), custom_call_target="tpu_custom_call", output_to_operand_aliasing={{}: (3, {})} | custom-call | tf_op jit(solution)/shard_map/store/pallas_call | solution.py:163
  25.5 0.8 %store.6.refs_1_ = bf16[128,4096]{1,0:T(8,128)(2,1)} custom-call(s32[8]{0:T(128)S(4)} %get-tuple-element.17.owner, bf16[128,512]{1,0:T(8,128)(2,1)S(1)} %collective-permute-done.7.refs_0_, bf16[128,512]{1,0:T(8,128)(2,1)S(1)} %collective-permute-done.9.refs_1_, bf16[128,512]{1,0:T(8,128)(2,1)S(1)} %collective-permute-done.5.refs_2_, ...), custom_call_target="tpu_custom_call", output_to_operand_aliasing={{}: (5, {})} | custom-call | tf_op jit(solution)/shard_map/store/pallas_call | solution.py:163
  26.3 0.7 %store.7 = bf16[128,4096]{1,0:T(8,128)(2,1)} custom-call(s32[8]{0:T(128)S(4)} %get-tuple-element.17.owner, bf16[128,512]{1,0:T(8,128)(2,1)S(1)} %collective-permute-done.6.refs_0_, bf16[128,4096]{1,0:T(8,128)(2,1)} %store.6.refs_1_), custom_call_target="tpu_custom_call", output_to_operand_aliasing={{}: (2, {})} | custom-call | tf_op jit(solution)/shard_map/store/pallas_call | solution.py:163
  (12 shorter events, 0.1 us)
Async XLA Ops:
  2.0 5.1 %collective-permute-start = (bf16[3,128,512]{2,1,0:T(8,128)(2,1)S(1)}, bf16[3,128,512]{2,1,0:T(8,128)(2,1)S(1)}, u32[]{:S(2)}, u32[]{:S(2)}) collective-permute-start(bf16[3,128,512]{2,1,0:T(8,128)(2,1)S(1)} %get-tuple-element.20), channel_id=1, source_target_pairs={{0,4},{4,0},{8,12},{12,8},{16,20},{20,16},{24,28},{28,24},{1,5},{5... | collective-permute-start | bytes 1179656 | tf_op jit(solution)/shard_map/ppermute | solution.py:35
  2.5 1.5 %collective-permute-start.1 = (bf16[128,512]{1,0:T(8,128)(2,1)S(1)}, bf16[128,512]{1,0:T(8,128)(2,1)S(1)}, u32[]{:S(2)}, u32[]{:S(2)}) collective-permute-start(bf16[128,512]{1,0:T(8,128)(2,1)S(1)} %get-tuple-element.22), channel_id=1, source_target_pairs={{0,4},{4,0},{8,12},{12,8},{16,20},{20,16},{24,28},{28,24},{1,5},{5... | collective-permute-start | bytes 393224 | tf_op jit(solution)/shard_map/ppermute | solution.py:35
  4.1 11.2 %copy-start = (f32[128,512]{1,0:T(8,128)S(1)}, f32[128,512]{1,0:T(8,128)}, u32[]{:S(2)}) copy-start(f32[128,512]{1,0:T(8,128)} %outer.1) | copy-start | bytes 786436
  4.1 11.2 %copy-start.1 = (f32[128,512]{1,0:T(8,128)S(1)}, f32[128,512]{1,0:T(8,128)}, u32[]{:S(2)}) copy-start(f32[128,512]{1,0:T(8,128)} %velocity.1) | copy-start | bytes 786436
  4.1 6.8 %collective-permute-start.2 = (bf16[128,512]{1,0:T(8,128)(2,1)S(1)}, bf16[128,512]{1,0:T(8,128)(2,1)S(1)}, u32[]{:S(2)}, u32[]{:S(2)}) collective-permute-start(bf16[128,512]{1,0:T(8,128)(2,1)S(1)} %sum_head.1), channel_id=1, source_target_pairs={{0,8},{4,12},{8,0},{12,4},{16,24},{20,28},{24,16},{28,20},{1,9},{5... | collective-permute-start | bytes 393224 | tf_op jit(solution)/shard_map/ppermute | solution.py:32
  7.2 8.1 %collective-permute-start.3 = (bf16[128,512]{1,0:T(8,128)(2,1)S(1)}, bf16[128,512]{1,0:T(8,128)(2,1)S(1)}, u32[]{:S(2)}, u32[]{:S(2)}) collective-permute-start(bf16[128,512]{1,0:T(8,128)(2,1)S(1)} %get-tuple-element.23), channel_id=1, source_target_pairs={{0,16},{4,20},{8,24},{12,28},{16,0},{20,4},{24,8},{28,12},{1,17},{... | collective-permute-start | bytes 393224 | tf_op jit(solution)/shard_map/ppermute | solution.py:32
  8.8 6.6 %collective-permute-start.4 = (bf16[128,512]{1,0:T(8,128)(2,1)S(1)}, bf16[128,512]{1,0:T(8,128)(2,1)S(1)}, u32[]{:S(2)}, u32[]{:S(2)}) collective-permute-start(bf16[128,512]{1,0:T(8,128)(2,1)S(1)} %get-tuple-element.24), channel_id=1, source_target_pairs={{0,24},{4,28},{8,16},{12,20},{16,8},{20,12},{24,0},{28,4},{1,25},{... | collective-permute-start | bytes 393224 | tf_op jit(solution)/shard_map/ppermute | solution.py:32
  15.5 6.4 %collective-permute-start.7 = (bf16[128,512]{1,0:T(8,128)(2,1)S(1)}, bf16[128,512]{1,0:T(8,128)(2,1)S(1)}, u32[]{:S(2)}, u32[]{:S(2)}) collective-permute-start(bf16[128,512]{1,0:T(8,128)(2,1)S(1)} %get-tuple-element.25.refs_0_), channel_id=1, source_target_pairs={{0,16},{4,20},{8,24},{12,28},{16,0},{20,4},{24,8},{28,12},{1,17},{... | collective-permute-start | bytes 393224 | tf_op jit(solution)/shard_map/ppermute | solution.py:32
  17.1 5.5 %collective-permute-start.8 = (bf16[128,512]{1,0:T(8,128)(2,1)S(1)}, bf16[128,512]{1,0:T(8,128)(2,1)S(1)}, u32[]{:S(2)}, u32[]{:S(2)}) collective-permute-start(bf16[128,512]{1,0:T(8,128)(2,1)S(1)} %get-tuple-element.25.refs_0_), channel_id=1, source_target_pairs={{0,8},{4,12},{8,0},{12,4},{16,24},{20,28},{24,16},{28,20},{1,9},{5... | collective-permute-start | bytes 393224 | tf_op jit(solution)/shard_map/ppermute | solution.py:32
  17.6 6.2 %collective-permute-start.5 = (bf16[128,512]{1,0:T(8,128)(2,1)S(1)}, bf16[128,512]{1,0:T(8,128)(2,1)S(1)}, u32[]{:S(2)}, u32[]{:S(2)}) collective-permute-start(bf16[128,512]{1,0:T(8,128)(2,1)S(1)} %get-tuple-element.25.refs_0_), channel_id=1, source_target_pairs={{0,24},{4,28},{8,16},{12,20},{16,8},{20,12},{24,0},{28,4},{1,25},{... | collective-permute-start | bytes 393224 | tf_op jit(solution)/shard_map/ppermute | solution.py:32
  19.0 5.7 %collective-permute-start.11 = (bf16[128,512]{1,0:T(8,128)(2,1)S(1)}, bf16[128,512]{1,0:T(8,128)(2,1)S(1)}, u32[]{:S(2)}, u32[]{:S(2)}) collective-permute-start(bf16[128,512]{1,0:T(8,128)(2,1)S(1)} %get-tuple-element.25.refs_0_), channel_id=1, source_target_pairs={{0,4},{4,0},{8,12},{12,8},{16,20},{20,16},{24,28},{28,24},{1,5},{5... | collective-permute-start | bytes 393224 | tf_op jit(solution)/shard_map/ppermute | solution.py:35
  21.9 3.5 %collective-permute-start.10 = (bf16[128,512]{1,0:T(8,128)(2,1)S(1)}, bf16[128,512]{1,0:T(8,128)(2,1)S(1)}, u32[]{:S(2)}, u32[]{:S(2)}) collective-permute-start(bf16[128,512]{1,0:T(8,128)(2,1)S(1)} %collective-permute-done.7.refs_0_), channel_id=1, source_target_pairs={{0,4},{4,0},{8,12},{12,8},{16,20},{20,16},{24,28},{28,24},{1,5},{5... | collective-permute-start | bytes 393224 | tf_op jit(solution)/shard_map/ppermute | solution.py:35
  22.6 2.9 %collective-permute-start.9 = (bf16[128,512]{1,0:T(8,128)(2,1)S(1)}, bf16[128,512]{1,0:T(8,128)(2,1)S(1)}, u32[]{:S(2)}, u32[]{:S(2)}) collective-permute-start(bf16[128,512]{1,0:T(8,128)(2,1)S(1)} %collective-permute-done.8.refs_0_), channel_id=1, source_target_pairs={{0,4},{4,0},{8,12},{12,8},{16,20},{20,16},{24,28},{28,24},{1,5},{5... | collective-permute-start | bytes 393224 | tf_op jit(solution)/shard_map/ppermute | solution.py:35
  23.8 2.5 %collective-permute-start.6 = (bf16[128,512]{1,0:T(8,128)(2,1)S(1)}, bf16[128,512]{1,0:T(8,128)(2,1)S(1)}, u32[]{:S(2)}, u32[]{:S(2)}) collective-permute-start(bf16[128,512]{1,0:T(8,128)(2,1)S(1)} %collective-permute-done.5.refs_2_), channel_id=1, source_target_pairs={{0,4},{4,0},{8,12},{12,8},{16,20},{20,16},{24,28},{28,24},{1,5},{5... | collective-permute-start | bytes 393224 | tf_op jit(solution)/shard_map/ppermute | solution.py:35

commit v5 on v4

--- a/solution.py
+++ b/solution.py
@@ -27,9 +27,10 @@
     width = deltas.shape[2] // groups
     bf16, f32 = jnp.bfloat16, jnp.float32
     flips = sorted(range(chips), key=lambda m: (m.bit_count(), m))
+    back = sorted(range(chips), key=lambda m: (m.bit_count(), -m))
 
-    def direct(x, s):
-        return lax.ppermute(x, "rep", [(i, i ^ 2 * flips[s]) for i in range(groups)])
+    def direct(x, s, order):
+        return lax.ppermute(x, "rep", [(i, i ^ 2 * order[s]) for i in range(groups)])
 
     def swap(x):
         return lax.ppermute(x, "rep", [(i, i ^ 1) for i in range(groups)])
@@ -104,7 +105,7 @@
         out_shape=tile(),
         name="sum_head",
     )(owner_of, presence, whole, vmem(head))
-    terms = [direct(head, 1)]
+    terms = [direct(head, 1, flips)]
     *sums, own_sum = pl.pallas_call(
         sum_tail,
         in_specs=[SMEM] * 2 + [VMEM] * 2,
@@ -113,7 +114,7 @@
         name="sum_tail",
     )(owner_of, presence, whole, vmem(tail))
     for s, x in enumerate(sums, 2):
-        terms.append(direct(x, s))
+        terms.append(direct(x, s, flips))
 
     def update(flag, outer, velocity, *refs):
         ins, (ship, next_outer, next_velocity) = refs[:chips], refs[chips:]
@@ -135,7 +136,7 @@
 
     got = [shipped]
     for s in range(1, chips):
-        got.append(direct(shipped, s))
+        got.append(direct(shipped, s, back))
     other = [swap(shipped)]
     for s in range(1, chips):
         other.append(swap(got[s]))
@@ -152,7 +153,7 @@
             chip, core = where()
             pieces = list(zip(wholes, outs))
             for x, (_, side, s) in zip(ins, plan):
-                at = device(chip, 1 - core if side else core, s)
+                at = (chip ^ back[s]) * 2 + (1 - core if side else core)
                 pieces.append((x, out.at[:, columns(owner, at)]))
             copies = [pltpu.make_async_copy(a, b, sem.at[i]) for i, (a, b) in enumerate(pieces)]
             for copy in copies:
@@ -175,9 +176,9 @@
     for s in range(1, tail):
         plan = [(got[s], False, s), *((other[k], True, k) for k in range(s - 1, s))]
         if s == tail - 1:
-            plan += [(got[tail], False, tail), *((other[k], True, k) for k in range(tail - 1, tail))]
+            plan += [(got[tail], False, tail)]
         (new_weights,) = store(plan, new_weights)
-    (new_weights,) = store([(other[tail], True, tail)], new_weights)
+    (new_weights,) = store([(other[k], True, k) for k in (tail - 1, tail)], new_weights)
     return (new_weights, new_outer, new_momentum)
 
 

time: 27.2 us -> 27.2 us (level)
  no operation moved by 1% of the time
where the time goes in v5:
time: 27.2 us; the launch traced here: 27 us
  waiting for transfers between devices  12.8 us (47%)
  starting transfers between devices  8.75 us (32%)
  Pallas kernels  4.78 us (18%)
  between operations  0.74 us (3%)
    ppermute x6, waiting for transfers between devices, direct(): lax.ppermute(x, 'rep', [(i, i ^ 2 * order[s]) for i in range(groups)])  11.3 us
    ppermute x6, starting transfers between devices, direct(): lax.ppermute(x, 'rep', [(i, i ^ 2 * order[s]) for i in range(groups)])  8.1 us
    pallas_call x4, Pallas kernels, store(): pl.pallas_call(body, in_specs=[SMEM] + [VMEM] * (len(arrays) + len(extra)...  3.13 us
    ppermute x6, waiting for transfers between devices, swap(): return lax.ppermute(x, 'rep', [(i, i ^ 1) for i in range(groups)])  1.47 us
    pallas_call x1, Pallas kernels, shards(): pl.pallas_call(load, in_specs=[ANY] * 3, out_specs=[SMEM] * 2 + [VMEM] *...  1.34 us
    ppermute x6, starting transfers between devices, swap(): return lax.ppermute(x, 'rep', [(i, i ^ 1) for i in range(groups)])  0.65 us
  transfers between devices with their start and end apart: 12, of which 6 were waited for; matrix products, arithmetic and copies ran while one was open for 0% of the time, Pallas kernels for 10%

profile of v5, /device:TPU:0, one launch (start us, length us, event | category | flops | bytes accessed | tf_op | source)
XLA Modules:
  0.0 27.0 jit_solution(15012688726815783443)
XLA Ops:
  0.6 1.3 %load.1 = (s32[8]{0:T(128)S(4)}, s32[8]{0:T(128)S(4)}, bf16[128,4096]{1,0:T(8,128)(2,1)S(1)}, bf16[128,512]{1,0:T(8,128)(2,1)S(1)}, bf16[3,128,512]{2,1,0:T(8,128)(2,1)S(1)}) custom-call(s32[8]{0:T(128)} %owner_hbm.1, s32[8]{0:T(128)} %flag_hbm.1, bf16[1,128,4096]{2,1,0:T(8,128)(2,1)} %delta.1), custom_call_target="tpu_custom_call" | custom-call | tf_op jit(solution)/shard_map/load/pallas_call | solution.py:76
  2.0 0.6 %collective-permute-start = (bf16[3,128,512]{2,1,0:T(8,128)(2,1)S(1)}, bf16[3,128,512]{2,1,0:T(8,128)(2,1)S(1)}, u32[]{:S(2)}, u32[]{:S(2)}) collective-permute-start(bf16[3,128,512]{2,1,0:T(8,128)(2,1)S(1)} %get-tuple-element.20), channel_id=1, source_target_pairs={{0,4},{4,0},{8,12},{12,8},{16,20},{20,16},{24,28},{28,24},{1,5},{5... | collective-permute-start | bytes 1179656 | tf_op jit(solution)/shard_map/ppermute | solution.py:36
  2.5 0.1 collective-permute-start.1
  2.6 1.5 %collective-permute-done.1.got = bf16[128,512]{1,0:T(8,128)(2,1)S(1)} collective-permute-done((bf16[128,512]{1,0:T(8,128)(2,1)S(1)}, bf16[128,512]{1,0:T(8,128)(2,1)S(1)}, u32[]{:S(2)}, u32[]{:S(2)}) %collective-permute-start.1) | collective-permute-done | bytes 131104 | tf_op jit(solution)/shard_map/ppermute | solution.py:36
  4.1 0.0 copy-start
  4.1 0.0 copy-start.1
  4.1 2.9 %collective-permute-start.2 = (bf16[128,512]{1,0:T(8,128)(2,1)S(1)}, bf16[128,512]{1,0:T(8,128)(2,1)S(1)}, u32[]{:S(2)}, u32[]{:S(2)}) collective-permute-start(bf16[128,512]{1,0:T(8,128)(2,1)S(1)} %sum_head.1), channel_id=1, source_target_pairs={{0,8},{4,12},{8,0},{12,4},{16,24},{20,28},{24,16},{28,20},{1,9},{5... | collective-permute-start | bytes 393224 | tf_op jit(solution)/shard_map/ppermute | solution.py:33
  7.1 0.1 sum_tail.1
  7.2 1.6 %collective-permute-start.3 = (bf16[128,512]{1,0:T(8,128)(2,1)S(1)}, bf16[128,512]{1,0:T(8,128)(2,1)S(1)}, u32[]{:S(2)}, u32[]{:S(2)}) collective-permute-start(bf16[128,512]{1,0:T(8,128)(2,1)S(1)} %get-tuple-element.23), channel_id=1, source_target_pairs={{0,16},{4,20},{8,24},{12,28},{16,0},{20,4},{24,8},{28,12},{1,17},{... | collective-permute-start | bytes 393224 | tf_op jit(solution)/shard_map/ppermute | solution.py:33
  8.8 0.0 collective-permute-start.4
  8.8 2.1 %collective-permute-done.2.refs_1_ = bf16[128,512]{1,0:T(8,128)(2,1)S(1)} collective-permute-done((bf16[128,512]{1,0:T(8,128)(2,1)S(1)}, bf16[128,512]{1,0:T(8,128)(2,1)S(1)}, u32[]{:S(2)}, u32[]{:S(2)}) %collective-permute-start.2) | collective-permute-done | bytes 131104 | tf_op jit(solution)/shard_map/ppermute | solution.py:33
  10.9 4.4 %collective-permute-done.3.refs_2_ = bf16[128,512]{1,0:T(8,128)(2,1)S(1)} collective-permute-done((bf16[128,512]{1,0:T(8,128)(2,1)S(1)}, bf16[128,512]{1,0:T(8,128)(2,1)S(1)}, u32[]{:S(2)}, u32[]{:S(2)}) %collective-permute-start.3) | collective-permute-done | bytes 131104 | tf_op jit(solution)/shard_map/ppermute | solution.py:33
  15.3 0.0 collective-permute-done.4.refs_3_
  15.3 0.1 update.1
  15.5 1.6 %collective-permute-start.9 = (bf16[128,512]{1,0:T(8,128)(2,1)S(1)}, bf16[128,512]{1,0:T(8,128)(2,1)S(1)}, u32[]{:S(2)}, u32[]{:S(2)}) collective-permute-start(bf16[128,512]{1,0:T(8,128)(2,1)S(1)} %get-tuple-element.25.refs_0_), channel_id=1, source_target_pairs={{0,16},{4,20},{8,24},{12,28},{16,0},{20,4},{24,8},{28,12},{1,17},{... | collective-permute-start | bytes 393224 | tf_op jit(solution)/shard_map/ppermute | solution.py:33
  17.1 0.5 %collective-permute-start.5 = (bf16[128,512]{1,0:T(8,128)(2,1)S(1)}, bf16[128,512]{1,0:T(8,128)(2,1)S(1)}, u32[]{:S(2)}, u32[]{:S(2)}) collective-permute-start(bf16[128,512]{1,0:T(8,128)(2,1)S(1)} %get-tuple-element.25.refs_0_), channel_id=1, source_target_pairs={{0,8},{4,12},{8,0},{12,4},{16,24},{20,28},{24,16},{28,20},{1,9},{5... | collective-permute-start | bytes 393224 | tf_op jit(solution)/shard_map/ppermute | solution.py:33
  17.6 1.4 %collective-permute-start.7 = (bf16[128,512]{1,0:T(8,128)(2,1)S(1)}, bf16[128,512]{1,0:T(8,128)(2,1)S(1)}, u32[]{:S(2)}, u32[]{:S(2)}) collective-permute-start(bf16[128,512]{1,0:T(8,128)(2,1)S(1)} %get-tuple-element.25.refs_0_), channel_id=1, source_target_pairs={{0,24},{4,28},{8,16},{12,20},{16,8},{20,12},{24,0},{28,4},{1,25},{... | collective-permute-start | bytes 393224 | tf_op jit(solution)/shard_map/ppermute | solution.py:33
  19.0 2.9 %collective-permute-done.9.refs_0_ = bf16[128,512]{1,0:T(8,128)(2,1)S(1)} collective-permute-done((bf16[128,512]{1,0:T(8,128)(2,1)S(1)}, bf16[128,512]{1,0:T(8,128)(2,1)S(1)}, u32[]{:S(2)}, u32[]{:S(2)}) %collective-permute-start.9) | collective-permute-done | bytes 131104 | tf_op jit(solution)/shard_map/ppermute | solution.py:33
  21.9 0.7 %collective-permute-done.5.refs_0_ = bf16[128,512]{1,0:T(8,128)(2,1)S(1)} collective-permute-done((bf16[128,512]{1,0:T(8,128)(2,1)S(1)}, bf16[128,512]{1,0:T(8,128)(2,1)S(1)}, u32[]{:S(2)}, u32[]{:S(2)}) %collective-permute-start.5) | collective-permute-done | bytes 131104 | tf_op jit(solution)/shard_map/ppermute | solution.py:33
  22.6 1.2 %collective-permute-done.7.refs_2_ = bf16[128,512]{1,0:T(8,128)(2,1)S(1)} collective-permute-done((bf16[128,512]{1,0:T(8,128)(2,1)S(1)}, bf16[128,512]{1,0:T(8,128)(2,1)S(1)}, u32[]{:S(2)}, u32[]{:S(2)}) %collective-permute-start.7) | collective-permute-done | bytes 131104 | tf_op jit(solution)/shard_map/ppermute | solution.py:33
  23.8 0.9 %store.4 = (bf16[128,4096]{1,0:T(8,128)(2,1)}, f32[128,512]{1,0:T(8,128)}, f32[128,512]{1,0:T(8,128)}) custom-call(s32[8]{0:T(128)S(4)} %get-tuple-element.17.owner, bf16[128,512]{1,0:T(8,128)(2,1)S(1)} %get-tuple-element.25.refs_0_, f32[128,512]{1,0:T(8,128)S(1)} %get-tuple-element.26.refs_1_, f32[128,512]{1,0:T(8,128)S(1)} %get-tuple-element.27.refs_2_), custom_call_target="tpu_custom_call" | custom-call | tf_op jit(solution)/shard_map/store/pallas_call | solution.py:164
  24.7 0.7 %store.5.refs_3_ = bf16[128,4096]{1,0:T(8,128)(2,1)} custom-call(s32[8]{0:T(128)S(4)} %get-tuple-element.17.owner, bf16[128,512]{1,0:T(8,128)(2,1)S(1)} %collective-permute-done.9.refs_0_, bf16[128,512]{1,0:T(8,128)(2,1)S(1)} %collective-permute-done.11.refs_1_, bf16[128,4096]{1,0:T(8,128)(2,1)} %get-tuple-element.28.refs_2_), custom_call_target="tpu_custom_call", output_to_operand_aliasing={{}: (3, {})} | custom-call | tf_op jit(solution)/shard_map/store/pallas_call | solution.py:164
  25.5 0.8 %store.6.refs_2_ = bf16[128,4096]{1,0:T(8,128)(2,1)} custom-call(s32[8]{0:T(128)S(4)} %get-tuple-element.17.owner, bf16[128,512]{1,0:T(8,128)(2,1)S(1)} %collective-permute-done.5.refs_0_, bf16[128,512]{1,0:T(8,128)(2,1)S(1)} %collective-permute-done.10.refs_1_, bf16[128,512]{1,0:T(8,128)(2,1)S(1)} %collective-permute-done.7.refs_2_, ...), custom_call_target="tpu_custom_call", output_to_operand_aliasing={{}: (4, {})} | custom-call | tf_op jit(solution)/shard_map/store/pallas_call | solution.py:164
  26.3 0.7 %store.7 = bf16[128,4096]{1,0:T(8,128)(2,1)} custom-call(s32[8]{0:T(128)S(4)} %get-tuple-element.17.owner, bf16[128,512]{1,0:T(8,128)(2,1)S(1)} %collective-permute-done.6.refs_0_, bf16[128,512]{1,0:T(8,128)(2,1)S(1)} %collective-permute-done.8.refs_1_, bf16[128,4096]{1,0:T(8,128)(2,1)} %store.6.refs_2_), custom_call_target="tpu_custom_call", output_to_operand_aliasing={{}: (3, {})} | custom-call | tf_op jit(solution)/shard_map/store/pallas_call | solution.py:164
  (12 shorter events, 0.1 us)
Async XLA Ops:
  2.0 5.1 %collective-permute-start = (bf16[3,128,512]{2,1,0:T(8,128)(2,1)S(1)}, bf16[3,128,512]{2,1,0:T(8,128)(2,1)S(1)}, u32[]{:S(2)}, u32[]{:S(2)}) collective-permute-start(bf16[3,128,512]{2,1,0:T(8,128)(2,1)S(1)} %get-tuple-element.20), channel_id=1, source_target_pairs={{0,4},{4,0},{8,12},{12,8},{16,20},{20,16},{24,28},{28,24},{1,5},{5... | collective-permute-start | bytes 1179656 | tf_op jit(solution)/shard_map/ppermute | solution.py:36
  2.5 1.5 %collective-permute-start.1 = (bf16[128,512]{1,0:T(8,128)(2,1)S(1)}, bf16[128,512]{1,0:T(8,128)(2,1)S(1)}, u32[]{:S(2)}, u32[]{:S(2)}) collective-permute-start(bf16[128,512]{1,0:T(8,128)(2,1)S(1)} %get-tuple-element.22), channel_id=1, source_target_pairs={{0,4},{4,0},{8,12},{12,8},{16,20},{20,16},{24,28},{28,24},{1,5},{5... | collective-permute-start | bytes 393224 | tf_op jit(solution)/shard_map/ppermute | solution.py:36
  4.1 11.2 %copy-start = (f32[128,512]{1,0:T(8,128)S(1)}, f32[128,512]{1,0:T(8,128)}, u32[]{:S(2)}) copy-start(f32[128,512]{1,0:T(8,128)} %outer.1) | copy-start | bytes 786436
  4.1 11.2 %copy-start.1 = (f32[128,512]{1,0:T(8,128)S(1)}, f32[128,512]{1,0:T(8,128)}, u32[]{:S(2)}) copy-start(f32[128,512]{1,0:T(8,128)} %velocity.1) | copy-start | bytes 786436
  4.1 6.8 %collective-permute-start.2 = (bf16[128,512]{1,0:T(8,128)(2,1)S(1)}, bf16[128,512]{1,0:T(8,128)(2,1)S(1)}, u32[]{:S(2)}, u32[]{:S(2)}) collective-permute-start(bf16[128,512]{1,0:T(8,128)(2,1)S(1)} %sum_head.1), channel_id=1, source_target_pairs={{0,8},{4,12},{8,0},{12,4},{16,24},{20,28},{24,16},{28,20},{1,9},{5... | collective-permute-start | bytes 393224 | tf_op jit(solution)/shard_map/ppermute | solution.py:33
  7.2 8.1 %collective-permute-start.3 = (bf16[128,512]{1,0:T(8,128)(2,1)S(1)}, bf16[128,512]{1,0:T(8,128)(2,1)S(1)}, u32[]{:S(2)}, u32[]{:S(2)}) collective-permute-start(bf16[128,512]{1,0:T(8,128)(2,1)S(1)} %get-tuple-element.23), channel_id=1, source_target_pairs={{0,16},{4,20},{8,24},{12,28},{16,0},{20,4},{24,8},{28,12},{1,17},{... | collective-permute-start | bytes 393224 | tf_op jit(solution)/shard_map/ppermute | solution.py:33
  8.8 6.6 %collective-permute-start.4 = (bf16[128,512]{1,0:T(8,128)(2,1)S(1)}, bf16[128,512]{1,0:T(8,128)(2,1)S(1)}, u32[]{:S(2)}, u32[]{:S(2)}) collective-permute-start(bf16[128,512]{1,0:T(8,128)(2,1)S(1)} %get-tuple-element.24), channel_id=1, source_target_pairs={{0,24},{4,28},{8,16},{12,20},{16,8},{20,12},{24,0},{28,4},{1,25},{... | collective-permute-start | bytes 393224 | tf_op jit(solution)/shard_map/ppermute | solution.py:33
  15.5 6.4 %collective-permute-start.9 = (bf16[128,512]{1,0:T(8,128)(2,1)S(1)}, bf16[128,512]{1,0:T(8,128)(2,1)S(1)}, u32[]{:S(2)}, u32[]{:S(2)}) collective-permute-start(bf16[128,512]{1,0:T(8,128)(2,1)S(1)} %get-tuple-element.25.refs_0_), channel_id=1, source_target_pairs={{0,16},{4,20},{8,24},{12,28},{16,0},{20,4},{24,8},{28,12},{1,17},{... | collective-permute-start | bytes 393224 | tf_op jit(solution)/shard_map/ppermute | solution.py:33
  17.1 5.5 %collective-permute-start.5 = (bf16[128,512]{1,0:T(8,128)(2,1)S(1)}, bf16[128,512]{1,0:T(8,128)(2,1)S(1)}, u32[]{:S(2)}, u32[]{:S(2)}) collective-permute-start(bf16[128,512]{1,0:T(8,128)(2,1)S(1)} %get-tuple-element.25.refs_0_), channel_id=1, source_target_pairs={{0,8},{4,12},{8,0},{12,4},{16,24},{20,28},{24,16},{28,20},{1,9},{5... | collective-permute-start | bytes 393224 | tf_op jit(solution)/shard_map/ppermute | solution.py:33
  17.6 6.2 %collective-permute-start.7 = (bf16[128,512]{1,0:T(8,128)(2,1)S(1)}, bf16[128,512]{1,0:T(8,128)(2,1)S(1)}, u32[]{:S(2)}, u32[]{:S(2)}) collective-permute-start(bf16[128,512]{1,0:T(8,128)(2,1)S(1)} %get-tuple-element.25.refs_0_), channel_id=1, source_target_pairs={{0,24},{4,28},{8,16},{12,20},{16,8},{20,12},{24,0},{28,4},{1,25},{... | collective-permute-start | bytes 393224 | tf_op jit(solution)/shard_map/ppermute | solution.py:33
  19.0 5.7 %collective-permute-start.11 = (bf16[128,512]{1,0:T(8,128)(2,1)S(1)}, bf16[128,512]{1,0:T(8,128)(2,1)S(1)}, u32[]{:S(2)}, u32[]{:S(2)}) collective-permute-start(bf16[128,512]{1,0:T(8,128)(2,1)S(1)} %get-tuple-element.25.refs_0_), channel_id=1, source_target_pairs={{0,4},{4,0},{8,12},{12,8},{16,20},{20,16},{24,28},{28,24},{1,5},{5... | collective-permute-start | bytes 393224 | tf_op jit(solution)/shard_map/ppermute | solution.py:36
  21.9 3.5 %collective-permute-start.10 = (bf16[128,512]{1,0:T(8,128)(2,1)S(1)}, bf16[128,512]{1,0:T(8,128)(2,1)S(1)}, u32[]{:S(2)}, u32[]{:S(2)}) collective-permute-start(bf16[128,512]{1,0:T(8,128)(2,1)S(1)} %collective-permute-done.9.refs_0_), channel_id=1, source_target_pairs={{0,4},{4,0},{8,12},{12,8},{16,20},{20,16},{24,28},{28,24},{1,5},{5... | collective-permute-start | bytes 393224 | tf_op jit(solution)/shard_map/ppermute | solution.py:36
  22.6 3.7 %collective-permute-start.6 = (bf16[128,512]{1,0:T(8,128)(2,1)S(1)}, bf16[128,512]{1,0:T(8,128)(2,1)S(1)}, u32[]{:S(2)}, u32[]{:S(2)}) collective-permute-start(bf16[128,512]{1,0:T(8,128)(2,1)S(1)} %collective-permute-done.5.refs_0_), channel_id=1, source_target_pairs={{0,4},{4,0},{8,12},{12,8},{16,20},{20,16},{24,28},{28,24},{1,5},{5... | collective-permute-start | bytes 393224 | tf_op jit(solution)/shard_map/ppermute | solution.py:36
  23.8 2.4 %collective-permute-start.8 = (bf16[128,512]{1,0:T(8,128)(2,1)S(1)}, bf16[128,512]{1,0:T(8,128)(2,1)S(1)}, u32[]{:S(2)}, u32[]{:S(2)}) collective-permute-start(bf16[128,512]{1,0:T(8,128)(2,1)S(1)} %collective-permute-done.7.refs_2_), channel_id=1, source_target_pairs={{0,4},{4,0},{8,12},{12,8},{16,20},{20,16},{24,28},{28,24},{1,5},{5... | collective-permute-start | bytes 393224 | tf_op jit(solution)/shard_map/ppermute | solution.py:36
